TPU v7x, 8 devices: a whole 2x2x1 slice. The times are simulated.
8 devices in a mesh: dp: 1 (over z), tp: 2 (over y), cp: 4 (over x, core).
Axes of the slice: x: 2, y: 2, z: 1, core: 2. Of those that a mesh axis runs over, the one named last changes fastest.
Arguments:
- x_in: bfloat16 [4096, 8192], P(('dp', 'cp', 'tp'))
- seg_ids: int32 [4096], P(('dp', 'cp', 'tp'))
- w_q: bfloat16 [8192, 64, 128], P(None, 'tp')
- w_k: bfloat16 [8192, 64, 128], P(None, 'tp')
- w_v: bfloat16 [8192, 64, 128], P(None, 'tp')
- w_o: bfloat16 [64, 128, 8192], P('tp')
Outputs:
- output: bfloat16 [4096, 8192], P(('dp', 'cp', 'tp'))
All inputs are finite; a program needn't handle non-finite values.
Results may differ from a plain program's by a relative error of at most 0.00426498.
Values are sent between devices in bfloat16 or wider.
A program may use at most 1.25 GiB of HBM per device.

v0:
```python
import jax
import jax.numpy as jnp
from jax import lax
from jax.sharding import PartitionSpec as P

NEG_BIG = -1e30


def block_update(softmax_state, q_blk, k_blk, v_blk, allowed, logit_scale):
    m_old, l_old, acc_old = softmax_state
    scores = jnp.einsum("qkge,ske->kgqs", q_blk, k_blk, preferred_element_type=jnp.float32) * logit_scale
    scores = jnp.where(allowed, scores, NEG_BIG)
    m_new = jnp.maximum(m_old, jnp.max(scores, axis=-1))
    prob_blk = jnp.exp(scores - m_new[..., None])
    rescale = jnp.exp(m_old - m_new)
    pv_part = jnp.einsum("kgqs,ske->kgqe", prob_blk.astype(jnp.bfloat16), v_blk, preferred_element_type=jnp.float32)
    return m_new, rescale * l_old + jnp.sum(prob_blk, axis=-1), rescale[..., None] * acc_old + pv_part


def visible_mask(pos_q, seg_q, pos_k, seg_k):
    return (seg_q[:, None] == seg_k[None, :]) & (pos_k[None, :] <= pos_q[:, None])


def solution(mesh):
    n_cp = mesh.shape["cp"]
    next_perm = [(dev_idx, (dev_idx + 1) % n_cp) for dev_idx in range(n_cp)]

    def per_device(x_loc, seg_loc, w_q, w_k, w_v, w_o):
        cp_rank = lax.axis_index("cp")
        x_rows = lax.all_gather(x_loc, "tp", axis=0, tiled=True)
        seg_rows = lax.all_gather(seg_loc, "tp", axis=0, tiled=True)
        n_rows = x_rows.shape[0]
        piece_len = n_rows // 2
        kv_loc = w_k.shape[1]
        head_dim = w_k.shape[2]
        q_per_kv = w_q.shape[1] // kv_loc
        logit_scale = head_dim ** -0.5
        q_rows = jnp.einsum("sd,dhe->she", x_rows, w_q, preferred_element_type=jnp.float32).astype(jnp.bfloat16).reshape(n_rows, kv_loc, q_per_kv, head_dim)
        k_rows = jnp.einsum("sd,dhe->she", x_rows, w_k, preferred_element_type=jnp.float32).astype(jnp.bfloat16)
        v_rows = jnp.einsum("sd,dhe->she", x_rows, w_v, preferred_element_type=jnp.float32).astype(jnp.bfloat16)
        local_idx = jnp.arange(n_rows)

        def piece_positions(owner_rank):
            return jnp.where(local_idx < piece_len, owner_rank * piece_len + local_idx, (2 * n_cp - 1 - owner_rank) * piece_len + local_idx - piece_len)

        pos_q = piece_positions(cp_rank)
        late_q = q_rows[piece_len:]
        late_pos = pos_q[piece_len:]
        late_seg = seg_rows[piece_len:]
        state_shape = (kv_loc, q_per_kv, n_rows)
        init_state = (jnp.full(state_shape, NEG_BIG, jnp.float32), jnp.zeros(state_shape, jnp.float32), jnp.zeros(state_shape + (head_dim,), jnp.float32))
        first_state = block_update(init_state, q_rows, k_rows, v_rows, visible_mask(pos_q, seg_rows, pos_q, seg_rows), logit_scale)

        def kv_step(step_idx, loop_carry):
            k_cur, v_cur, seg_cur, softmax_state = loop_carry
            k_cur = lax.ppermute(k_cur, "cp", next_perm)
            v_cur = lax.ppermute(v_cur, "cp", next_perm)
            seg_cur = lax.ppermute(seg_cur, "cp", next_perm)
            src_rank = (cp_rank - step_idx) % n_cp
            pos_k = piece_positions(src_rank)

            def from_earlier(old_state):
                return block_update(old_state, q_rows, k_cur[:piece_len], v_cur[:piece_len], visible_mask(pos_q, seg_rows, pos_k[:piece_len], seg_cur[:piece_len]), logit_scale)

            def from_later(old_state):
                m_old, l_old, acc_old = old_state
                late_state = block_update((m_old[..., piece_len:], l_old[..., piece_len:], acc_old[:, :, piece_len:]), late_q, k_cur, v_cur, visible_mask(late_pos, late_seg, pos_k, seg_cur), logit_scale)
                return (jnp.concatenate([m_old[..., :piece_len], late_state[0]], axis=-1),
                        jnp.concatenate([l_old[..., :piece_len], late_state[1]], axis=-1),
                        jnp.concatenate([acc_old[:, :, :piece_len], late_state[2]], axis=2))

            new_state = lax.cond(src_rank < cp_rank, from_earlier, from_later, softmax_state)
            return k_cur, v_cur, seg_cur, new_state

        final_carry = lax.fori_loop(1, n_cp, kv_step, (k_rows, v_rows, seg_rows, first_state))
        l_fin = final_carry[3][1]
        acc_fin = final_carry[3][2]
        attn_out = (acc_fin / l_fin[..., None]).astype(jnp.bfloat16)
        y_part = jnp.einsum("kgqe,kged->qd", attn_out, w_o.reshape(kv_loc, q_per_kv, head_dim, -1), preferred_element_type=jnp.float32)
        return lax.psum_scatter(y_part, "tp", scatter_dimension=0, tiled=True).astype(jnp.bfloat16)

    return jax.shard_map(
        per_device,
        mesh=mesh,
        in_specs=(P(("dp", "cp", "tp"), None), P(("dp", "cp", "tp")), P(None, "tp", None), P(None, "tp", None), P(None, "tp", None), P("tp", None, None)),
        out_specs=P(("dp", "cp", "tp"), None),
        check_vma=False,
    )
```

profile of v0, /device:TPU:0, one launch (start us, length us, event | category | flops | bytes accessed | tf_op | source)
XLA Modules:
  0.0 1969.9 jit_solution(10510019524006200205)
XLA Ops:
  16.7 191.7 %all-gather.3.cloned.1.call-done = bf16[1024,8192]{1,0:T(8,128)(2,1)} async-done(((bf16[512,8192]{1,0:T(8,128)(2,1)}), bf16[1024,8192]{1,0:T(8,128)(2,1)}) %all-gather.3.cloned.1.call-update) | async-done | bytes 16777232 | tf_op jit(solution)/shard_map/all_gather | solution.py:30
  208.4 79.7 %fusion.69 = bf16[1024,32,128]{2,0,1:T(8,128)(2,1)} fusion(bf16[8192,32,128]{2,1,0:T(8,128)(2,1)} %param.12, bf16[1024,8192]{1,0:T(8,128)(2,1)} %all-gather.3.cloned.1.call-done), kind=kOutput, calls=%fused_computation.76 | convolution fusion | flops 68723671040 | bytes 92274688 | tf_op jit(solution)/shard_map/sd,dhe->she/dot_general | solution.py:38
  292.8 79.9 %fusion.59 = bf16[1024,32,128]{2,0,1:T(8,128)(2,1)} fusion(bf16[8192,32,128]{2,1,0:T(8,128)(2,1)} %param.13, bf16[1024,8192]{1,0:T(8,128)(2,1)} %all-gather.3.cloned.1.call-done), kind=kOutput, calls=%fused_computation.74 | convolution fusion | flops 68723671040 | bytes 92274688 | tf_op jit(solution)/shard_map/sd,dhe->she/dot_general | solution.py:39
  372.7 52.3 %fusion.42 = (f32[32,1024]{1,0:T(8,128)S(1)}, f32[32,1024,1024]{2,1,0:T(8,128)}) fusion(pred[1024,1024]{0,1:T(8,128)(4,1)S(1)} %copy-done.1, bf16[1024,32,128]{2,0,1:T(8,128)(2,1)} %fusion.59, bf16[1024,32,128]{2,0,1:T(8,128)(2,1)} %fusion.69), kind=kOutput, calls=%fused_computation.57 | convolution fusion | flops 8690565120 | bytes 152174592 | tf_op jit(solution)/shard_map/qkge,ske->kgqs/dot_general | solution.py:11
  425.7 41.6 %fusion.41 = f32[32,1024]{1,0:T(8,128)S(1)} fusion(f32[32,1024,1024]{2,1,0:T(8,128)} %get-tuple-element.580, f32[32,1024]{1,0:T(8,128)S(1)} %get-tuple-element.578, pred[1024,1024]{0,1:T(8,128)(4,1)S(1)} %copy-done.1), kind=kLoop, calls=%fused_computation.56 | loop fusion | flops 134184960 | bytes 135528448 | tf_op jit(solution)/shard_map/reduce_sum | solution.py:17
  468.0 79.7 %fusion.64 = bf16[1024,32,128]{2,0,1:T(8,128)(2,1)} fusion(bf16[8192,32,128]{2,1,0:T(8,128)(2,1)} %param.14, bf16[1024,8192]{1,0:T(8,128)(2,1)} %all-gather.3.cloned.1.call-done), kind=kOutput, calls=%fused_computation.75 | convolution fusion | flops 68723671040 | bytes 92274688 | tf_op jit(solution)/shard_map/sd,dhe->she/dot_general | solution.py:40
  547.7 58.5 %add_bitcast_fusion = f32[32,1,1024,128]{3,2,0,1:T(8,128)} fusion(bf16[1024,32,128]{2,0,1:T(8,128)(2,1)} %fusion.64, f32[32,1024,1024]{2,1,0:T(8,128)} %get-tuple-element.580, f32[32,1024]{1,0:T(8,128)S(1)} %get-tuple-element.578, pred[1024,1024]{0,1:T(8,128)(4,1)S(1)} %copy-done.1, f32[32,1024]{1,0:T(8,128)S(1)} %copy-done.6), kind=kOutput, calls=%fused_computation.72 | convolution fusion | flops 8728346624 | bytes 160694272 | tf_op jit(solution)/shard_map/kgqs,ske->kgqe/dot_general | solution.py:16
  606.2 888.8 %while.27 = (s32[]{:T(128)}, bf16[1024,32,128]{2,0,1:T(8,128)(2,1)}, bf16[1024,32,128]{2,0,1:T(8,128)(2,1)}, s32[1024]{0:T(1024)S(1)}, f32[32,1,1024]{2,0,1:T(8,...) while((s32[]{:T(128)}, ...), condition=%wide.region_9.10_spmd.clone.clone, body=%wide.region_2.9_spmd.clone.clone.sunk | while | flops 8784566272 | bytes 427755328 | solution.py:75
  608.1 181.2 %collective-permute-done.2 = s32[1024]{0:T(1024)S(1)} collective-permute-done((s32[1024]{0:T(1024)S(1)}, s32[1024]{0:T(1024)S(1)}, u32[]{:S(2)}, u32[]{:S(2)}) %collective-permute-start.2) | collective-permute-done | bytes 4128 | tf_op jit(solution)/shard_map/while/body/eval_jaxpr/ppermute | solution.py:58
  789.8 96.6 %conditional.4 = (f32[32,1,1024]{2,0,1:T(8,128)}, f32[32,1,1024]{2,0,1:T(8,128)S(1)}, f32[32,1,1024,128]{3,2,0,1:T(8,128)}) conditional(s32[]{:T(128)} %convert_element_type.72, (f32[32,1,1024]{2,0,1:T(8,128)S(1)}, s32[512]{0:T(512)S(1)}, s32[1024]{0:T(1024)S(1)}, s32[1024]{0:T(1024)S(1)}, s32[512]{0:T(512)S(1)}, ...), branch_computations={%region_3.5_spmd, %region_6.8_spmd} | conditional | flops 8784560128 | bytes 326774848 | solution.py:72
  790.7 28.1 %fusion.6 = (f32[32,512]{1,0:T(8,128)S(1)}, f32[32,1024,512]{2,1,0:T(8,128)}) fusion(pred[512,1024]{0,1:T(8,128)(4,1)S(1)} %compare_and_fusion, bf16[1024,32,128]{2,0,1:T(8,128)(2,1)} %get-tuple-element.406, bf16[512,32,1,128]{3,0,1,2:T(8,128)(2,1)} %get-tuple-element.407), kind=kOutput, calls=%fused_computation.6 | convolution fusion | flops 4345282560 | bytes 80281600 | tf_op jit(solution)/shard_map/while/body/eval_jaxpr/cond/branch_0_fun/qkge,ske->kgqs/dot_general | solution.py:11
  818.8 21.6 %fusion.5 = f32[32,512]{1,0:T(8,128)S(1)} fusion(f32[32,1024,512]{2,1,0:T(8,128)} %get-tuple-element.571, f32[32,512]{1,0:T(8,128)S(1)} %bitcast.139, pred[512,1024]{0,1:T(8,128)(4,1)S(1)} %compare_and_fusion), kind=kLoop, calls=%fused_computation.5 | loop fusion | flops 67092480 | bytes 67764224 | tf_op jit(solution)/shard_map/while/body/eval_jaxpr/cond/branch_0_fun/reduce_sum | solution.py:17
  841.2 33.5 %bitcast_add_fusion = f32[32,1,512,128]{3,2,0,1:T(8,128)} fusion(f32[32,1,1024,128]{3,2,0,1:T(8,128)} %get-tuple-element.409, f32[32,512]{1,0:T(8,128)S(1)} %get-tuple-element.563, bf16[1024,32,128]{2,0,1:T(8,128)(2,1)} %get-tuple-element.410, f32[32,1024,512]{2,1,0:T(8,128)} %get-tuple-element.571, f32[32,512]{1,0:T(8,128)S(1)} %bitcast.140, ...), kind=kOutput, calls=%fused_computation.11 | convolution fusion | flops 4366270464 | bytes 92930048 | tf_op jit(solution)/shard_map/while/body/eval_jaxpr/cond/branch_0_fun/kgqs,ske->kgqe/dot_general | solution.py:16
  902.7 182.7 %collective-permute-done.2 = s32[1024]{0:T(1024)S(1)} collective-permute-done((s32[1024]{0:T(1024)S(1)}, s32[1024]{0:T(1024)S(1)}, u32[]{:S(2)}, u32[]{:S(2)}) %collective-permute-start.2) | collective-permute-done | bytes 4128 | tf_op jit(solution)/shard_map/while/body/eval_jaxpr/ppermute | solution.py:58
  1086.0 96.6 %conditional.4 = (f32[32,1,1024]{2,0,1:T(8,128)}, f32[32,1,1024]{2,0,1:T(8,128)S(1)}, f32[32,1,1024,128]{3,2,0,1:T(8,128)}) conditional(s32[]{:T(128)} %convert_element_type.72, (f32[32,1,1024]{2,0,1:T(8,128)S(1)}, s32[512]{0:T(512)S(1)}, s32[1024]{0:T(1024)S(1)}, s32[1024]{0:T(1024)S(1)}, s32[512]{0:T(512)S(1)}, ...), branch_computations={%region_3.5_spmd, %region_6.8_spmd} | conditional | flops 8784560128 | bytes 326774848 | solution.py:72
  1086.9 28.1 %fusion.6 = (f32[32,512]{1,0:T(8,128)S(1)}, f32[32,1024,512]{2,1,0:T(8,128)}) fusion(pred[512,1024]{0,1:T(8,128)(4,1)S(1)} %compare_and_fusion, bf16[1024,32,128]{2,0,1:T(8,128)(2,1)} %get-tuple-element.406, bf16[512,32,1,128]{3,0,1,2:T(8,128)(2,1)} %get-tuple-element.407), kind=kOutput, calls=%fused_computation.6 | convolution fusion | flops 4345282560 | bytes 80281600 | tf_op jit(solution)/shard_map/while/body/eval_jaxpr/cond/branch_0_fun/qkge,ske->kgqs/dot_general | solution.py:11
  1137.3 33.5 %bitcast_add_fusion = f32[32,1,512,128]{3,2,0,1:T(8,128)} fusion(f32[32,1,1024,128]{3,2,0,1:T(8,128)} %get-tuple-element.409, f32[32,512]{1,0:T(8,128)S(1)} %get-tuple-element.563, bf16[1024,32,128]{2,0,1:T(8,128)(2,1)} %get-tuple-element.410, f32[32,1024,512]{2,1,0:T(8,128)} %get-tuple-element.571, f32[32,512]{1,0:T(8,128)S(1)} %bitcast.140, ...), kind=kOutput, calls=%fused_computation.11 | convolution fusion | flops 4366270464 | bytes 92930048 | tf_op jit(solution)/shard_map/while/body/eval_jaxpr/cond/branch_0_fun/kgqs,ske->kgqe/dot_general | solution.py:16
  1198.8 182.7 %collective-permute-done.2 = s32[1024]{0:T(1024)S(1)} collective-permute-done((s32[1024]{0:T(1024)S(1)}, s32[1024]{0:T(1024)S(1)}, u32[]{:S(2)}, u32[]{:S(2)}) %collective-permute-start.2) | collective-permute-done | bytes 4128 | tf_op jit(solution)/shard_map/while/body/eval_jaxpr/ppermute | solution.py:58
  1382.1 96.6 %conditional.4 = (f32[32,1,1024]{2,0,1:T(8,128)}, f32[32,1,1024]{2,0,1:T(8,128)S(1)}, f32[32,1,1024,128]{3,2,0,1:T(8,128)}) conditional(s32[]{:T(128)} %convert_element_type.72, (f32[32,1,1024]{2,0,1:T(8,128)S(1)}, s32[512]{0:T(512)S(1)}, s32[1024]{0:T(1024)S(1)}, s32[1024]{0:T(1024)S(1)}, s32[512]{0:T(512)S(1)}, ...), branch_computations={%region_3.5_spmd, %region_6.8_spmd} | conditional | flops 8784560128 | bytes 326774848 | solution.py:72
  1383.0 28.1 %fusion.6 = (f32[32,512]{1,0:T(8,128)S(1)}, f32[32,1024,512]{2,1,0:T(8,128)}) fusion(pred[512,1024]{0,1:T(8,128)(4,1)S(1)} %compare_and_fusion, bf16[1024,32,128]{2,0,1:T(8,128)(2,1)} %get-tuple-element.406, bf16[512,32,1,128]{3,0,1,2:T(8,128)(2,1)} %get-tuple-element.407), kind=kOutput, calls=%fused_computation.6 | convolution fusion | flops 4345282560 | bytes 80281600 | tf_op jit(solution)/shard_map/while/body/eval_jaxpr/cond/branch_0_fun/qkge,ske->kgqs/dot_general | solution.py:11
  1411.1 21.6 %fusion.5 = f32[32,512]{1,0:T(8,128)S(1)} fusion(f32[32,1024,512]{2,1,0:T(8,128)} %get-tuple-element.571, f32[32,512]{1,0:T(8,128)S(1)} %bitcast.139, pred[512,1024]{0,1:T(8,128)(4,1)S(1)} %compare_and_fusion), kind=kLoop, calls=%fused_computation.5 | loop fusion | flops 67092480 | bytes 67764224 | tf_op jit(solution)/shard_map/while/body/eval_jaxpr/cond/branch_0_fun/reduce_sum | solution.py:17
  1433.5 33.5 %bitcast_add_fusion = f32[32,1,512,128]{3,2,0,1:T(8,128)} fusion(f32[32,1,1024,128]{3,2,0,1:T(8,128)} %get-tuple-element.409, f32[32,512]{1,0:T(8,128)S(1)} %get-tuple-element.563, bf16[1024,32,128]{2,0,1:T(8,128)(2,1)} %get-tuple-element.410, f32[32,1024,512]{2,1,0:T(8,128)} %get-tuple-element.571, f32[32,512]{1,0:T(8,128)S(1)} %bitcast.140, ...), kind=kOutput, calls=%fused_computation.11 | convolution fusion | flops 4366270464 | bytes 92930048 | tf_op jit(solution)/shard_map/while/body/eval_jaxpr/cond/branch_0_fun/kgqs,ske->kgqe/dot_general | solution.py:16
  1495.0 93.7 %convolution_bitcast_fusion = f32[1024,8192]{1,0:T(8,128)} fusion(bf16[32,128,8192]{2,1,0:T(8,128)(2,1)} %param.15, f32[32,1,1024,128]{3,2,0,1:T(8,128)} %get-tuple-element.444, f32[32,1024]{1,0:T(8,128)S(1)} %bitcast.141), kind=kOutput, calls=%fused_computation.67 | convolution fusion | flops 68727865344 | bytes 117571584 | tf_op jit(solution)/shard_map/kgqe,kged->qd/dot_general | solution.py:79
  1588.7 365.2 %reduce-scatter.2.cloned.1.call-done = f32[512,8192]{1,0:T(8,128)} async-done(((f32[1024,8192]{1,0:T(8,128)}), f32[512,8192]{1,0:T(8,128)}) %reduce-scatter.2.cloned.1.call-update) | async-done | bytes 16777232 | tf_op jit(solution)/shard_map/reduce_scatter | solution.py:80
  (102 shorter events, 138.7 us)
Async XLA Ops:
  6.5 201.9 %all-gather.3.cloned.1.call-start = ((), (), s32[]{:S(2)}) async-start(), calls=%async_computation.1 | async-start | bytes 25165824 | tf_op jit(solution)/shard_map/all_gather | solution.py:30
  7.3 1946.7 %reduce-scatter.2.cloned.1.call-start = ((), (), s32[]{:S(2)}) async-start(), calls=%async_computation.2 | async-start | bytes 50331648 | tf_op jit(solution)/shard_map/reduce_scatter | solution.py:80
  13.5 274.6 %copy-start.4 = (s32[2,1,512]{2,1,0:T(1,128)}, s32[2,1,512]{2,1,0:T(1,128)S(1)}, u32[]{:S(2)}) copy-start(s32[2,1,512]{2,1,0:T(1,128)S(1)} %all-gather) | copy-start | bytes 12292
  292.8 79.9 %copy-start.1 = (pred[1024,1024]{0,1:T(8,128)(4,1)S(1)}, pred[1024,1024]{0,1:T(8,128)(4,1)}, u32[]{:S(2)}) copy-start(pred[1024,1024]{0,1:T(8,128)(4,1)} %compare_and_fusion.2) | copy-start | bytes 3145732
  468.0 79.7 %copy-start.6 = (f32[32,1024]{1,0:T(8,128)S(1)}, f32[32,1024]{1,0:T(8,128)}, u32[]{:S(2)}) copy-start(f32[32,1024]{1,0:T(8,128)} %get-tuple-element.576) | copy-start | bytes 393220
  547.7 58.5 %copy-start.2 = (f32[32,1,1024]{2,0,1:T(8,128)S(1)}, f32[32,1,1024]{2,0,1:T(8,128)}, u32[]{:S(2)}) copy-start(f32[32,1,1024]{2,0,1:T(8,128)} %get-tuple-element.688) | copy-start | bytes 393220
  547.7 58.5 %copy-start.3 = (f32[32,1,1024]{2,0,1:T(8,128)S(1)}, f32[32,1,1024]{2,0,1:T(8,128)}, u32[]{:S(2)}) copy-start(f32[32,1,1024]{2,0,1:T(8,128)} %bitcast_add_fusion.4) | copy-start | bytes 393220
  547.7 58.5 %copy-start.5 = (s32[2,1,512]{2,1,0:T(1,128)S(1)}, s32[2,1,512]{2,1,0:T(1,128)}, u32[]{:S(2)}) copy-start(s32[2,1,512]{2,1,0:T(1,128)} %copy-done.4) | copy-start | bytes 12292
  547.7 58.5 %copy-start.7 = (s32[512]{0:T(512)S(1)}, s32[512]{0:T(512)}, u32[]{:S(2)}) copy-start(s32[512]{0:T(512)} %slice.43) | copy-start | bytes 6148
  547.7 58.5 %copy-start.8 = (s32[1,1,512]{2,1,0:T(1,128)S(1)}, s32[1,1,512]{2,1,0:T(1,128)}, u32[]{:S(2)}) copy-start(s32[1,1,512]{2,1,0:T(1,128)} %slice.47) | copy-start | bytes 6148
  547.7 58.5 %copy-start.9 = (s32[1024]{0:T(1024)S(1)}, s32[1024]{0:T(1024)}, u32[]{:S(2)}) copy-start(s32[1024]{0:T(1024)} %copy.43) | copy-start | bytes 12292
  606.4 183.4 %collective-permute-start = (bf16[1024,32,128]{2,0,1:T(8,128)(2,1)}, bf16[1024,32,128]{2,0,1:T(8,128)(2,1)}, u32[]{:S(2)}, u32[]{:S(2)}) collective-permute-start(bf16[1024,32,128]{2,0,1:T(8,128)(2,1)} %get-tuple-element.707), channel_id=1, source_target_pairs={{0,1},{1,2},{2,3},{3,0},{4,5},{5,6},{6,7},{7,4}} | collective-permute-start | bytes 25165832 | tf_op jit(solution)/shard_map/while/body/eval_jaxpr/ppermute | solution.py:56
  606.4 183.4 %collective-permute-start.1 = (bf16[1024,32,128]{2,0,1:T(8,128)(2,1)}, bf16[1024,32,128]{2,0,1:T(8,128)(2,1)}, u32[]{:S(2)}, u32[]{:S(2)}) collective-permute-start(bf16[1024,32,128]{2,0,1:T(8,128)(2,1)} %get-tuple-element.708), channel_id=1, source_target_pairs={{0,1},{1,2},{2,3},{3,0},{4,5},{5,6},{6,7},{7,4}} | collective-permute-start | bytes 25165832 | tf_op jit(solution)/shard_map/while/body/eval_jaxpr/ppermute | solution.py:57
  608.0 181.2 %collective-permute-start.2 = (s32[1024]{0:T(1024)S(1)}, s32[1024]{0:T(1024)S(1)}, u32[]{:S(2)}, u32[]{:S(2)}) collective-permute-start(s32[1024]{0:T(1024)S(1)} %get-tuple-element.709), channel_id=1, source_target_pairs={{0,1},{1,2},{2,3},{3,0},{4,5},{5,6},{6,7},{7,4}} | collective-permute-start | bytes 12296 | tf_op jit(solution)/shard_map/while/body/eval_jaxpr/ppermute | solution.py:58
  874.7 5.8 copy-start
  887.4 15.2 copy-start.10
  902.6 183.4 %collective-permute-start = (bf16[1024,32,128]{2,0,1:T(8,128)(2,1)}, bf16[1024,32,128]{2,0,1:T(8,128)(2,1)}, u32[]{:S(2)}, u32[]{:S(2)}) collective-permute-start(bf16[1024,32,128]{2,0,1:T(8,128)(2,1)} %get-tuple-element.707), channel_id=1, source_target_pairs={{0,1},{1,2},{2,3},{3,0},{4,5},{5,6},{6,7},{7,4}} | collective-permute-start | bytes 25165832 | tf_op jit(solution)/shard_map/while/body/eval_jaxpr/ppermute | solution.py:56
  902.6 183.4 %collective-permute-start.1 = (bf16[1024,32,128]{2,0,1:T(8,128)(2,1)}, bf16[1024,32,128]{2,0,1:T(8,128)(2,1)}, u32[]{:S(2)}, u32[]{:S(2)}) collective-permute-start(bf16[1024,32,128]{2,0,1:T(8,128)(2,1)} %get-tuple-element.708), channel_id=1, source_target_pairs={{0,1},{1,2},{2,3},{3,0},{4,5},{5,6},{6,7},{7,4}} | collective-permute-start | bytes 25165832 | tf_op jit(solution)/shard_map/while/body/eval_jaxpr/ppermute | solution.py:57
  902.6 182.8 %collective-permute-start.2 = (s32[1024]{0:T(1024)S(1)}, s32[1024]{0:T(1024)S(1)}, u32[]{:S(2)}, u32[]{:S(2)}) collective-permute-start(s32[1024]{0:T(1024)S(1)} %get-tuple-element.709), channel_id=1, source_target_pairs={{0,1},{1,2},{2,3},{3,0},{4,5},{5,6},{6,7},{7,4}} | collective-permute-start | bytes 12296 | tf_op jit(solution)/shard_map/while/body/eval_jaxpr/ppermute | solution.py:58
  1183.5 15.2 copy-start.10
  1198.7 183.4 %collective-permute-start = (bf16[1024,32,128]{2,0,1:T(8,128)(2,1)}, bf16[1024,32,128]{2,0,1:T(8,128)(2,1)}, u32[]{:S(2)}, u32[]{:S(2)}) collective-permute-start(bf16[1024,32,128]{2,0,1:T(8,128)(2,1)} %get-tuple-element.707), channel_id=1, source_target_pairs={{0,1},{1,2},{2,3},{3,0},{4,5},{5,6},{6,7},{7,4}} | collective-permute-start | bytes 25165832 | tf_op jit(solution)/shard_map/while/body/eval_jaxpr/ppermute | solution.py:56
  1198.7 183.4 %collective-permute-start.1 = (bf16[1024,32,128]{2,0,1:T(8,128)(2,1)}, bf16[1024,32,128]{2,0,1:T(8,128)(2,1)}, u32[]{:S(2)}, u32[]{:S(2)}) collective-permute-start(bf16[1024,32,128]{2,0,1:T(8,128)(2,1)} %get-tuple-element.708), channel_id=1, source_target_pairs={{0,1},{1,2},{2,3},{3,0},{4,5},{5,6},{6,7},{7,4}} | collective-permute-start | bytes 25165832 | tf_op jit(solution)/shard_map/while/body/eval_jaxpr/ppermute | solution.py:57
  1198.7 182.8 %collective-permute-start.2 = (s32[1024]{0:T(1024)S(1)}, s32[1024]{0:T(1024)S(1)}, u32[]{:S(2)}, u32[]{:S(2)}) collective-permute-start(s32[1024]{0:T(1024)S(1)} %get-tuple-element.709), channel_id=1, source_target_pairs={{0,1},{1,2},{2,3},{3,0},{4,5},{5,6},{6,7},{7,4}} | collective-permute-start | bytes 12296 | tf_op jit(solution)/shard_map/while/body/eval_jaxpr/ppermute | solution.py:58
  1479.6 15.2 copy-start.10
  (2 other events, 11.5 us)
Sparse Core Ops, SparseCore 0:
  8.8 199.5 all-gather.2
  1588.9 364.9 reduce-scatter.1
where the time goes:
time: 1980 us; the launch traced here: 1970 us
  waiting for transfers between devices  1100 us (56%)
  matrix products  629 us (32%)
  other arithmetic  142 us (7%)
  local copies, waits for them, and re-layouts  73.8 us (4%)
    ppermute x3, waiting for transfers between devices, kv_step(): seg_cur = lax.ppermute(seg_cur, 'cp', next_perm)  547 us
    reduce_scatter x1, waiting for transfers between devices, per_device(): lax.psum_scatter(y_part, 'tp', scatter_dimension=0, tiled=True)  365 us
    all_gather x1, waiting for transfers between devices, per_device(): x_rows = lax.all_gather(x_loc, 'tp', axis=0, tiled=True)  192 us
    dot_general x4, matrix products, block_update(): jnp.einsum('kgqs,ske->kgqe', prob_blk.astype(jnp.bfloat16), v_blk, prefer...  159 us
    dot_general x4, matrix products, block_update(): jnp.einsum('qkge,ske->kgqs', q_blk, k_blk, preferred_element_type=jnp.flo...  137 us
    reduce_sum x4, other arithmetic, block_update(): jnp.sum(prob_blk, axis=-1)  106 us
    dot_general x1, matrix products, per_device(): jnp.einsum('kgqe,kged->qd', attn_out, w_o.reshape(kv_loc, q_per_kv, head_...  93.7 us
    dot_general x1, matrix products, per_device(): jnp.einsum('sd,dhe->she', x_rows, w_k, preferred_element_type=jnp.float32)  79.9 us
  transfers between devices with their start and end apart: 11, of which 5 were waited for; matrix products, arithmetic and copies ran while one was open for 0% of the time, Pallas kernels for 0%

commit v1 on v0

v1 whole, which is shorter than its diff:
```python
import functools
import math

import jax
import jax.numpy as jnp
from jax import lax
from jax.experimental import pallas as pl
from jax.experimental.pallas import tpu as pltpu
from jax.sharding import PartitionSpec as P


NEG_BIG = -1e30
N_CP = 4
PIECE = 512
X_CHUNKS = 2
Y_SPLITS = (512, 1024, 1024, 1024, 1024, 1024, 1024, 1024, 512)
SWAP = [(0, 1), (1, 0)]


def attn_kernel(meta_ref, start_ref, *refs, n_heads, chunk_rows, q_chunks, coef):
    n_parts = len(chunk_rows)
    n_k = N_CP * n_parts
    n_q = N_CP * len(q_chunks)
    k_refs, v_refs = refs[:n_k], refs[n_k:2 * n_k]
    q_refs = refs[2 * n_k:2 * n_k + n_q]
    o_ref = refs[2 * n_k + n_q]
    k_buf, v_buf, q_buf, m_ref, l_ref, acc_ref, sems = refs[2 * n_k + n_q + 1:]
    head = pl.program_id(0)

    def copies(head_idx, slot):
        out = []
        for src in range(N_CP):
            for part, (kind, row0, rows) in enumerate(chunk_rows):
                piece = meta_ref[kind * N_CP + src]
                dst = pl.ds(pl.multiple_of(piece * PIECE + row0, 128), rows)
                idx = src * n_parts + part
                out.append(pltpu.make_async_copy(k_refs[idx].at[head_idx], k_buf.at[slot, dst], sems.at[slot]))
                out.append(pltpu.make_async_copy(v_refs[idx].at[head_idx], v_buf.at[slot, dst], sems.at[slot]))
            for part, (row0, rows) in enumerate(q_chunks):
                idx = src * len(q_chunks) + part
                out.append(pltpu.make_async_copy(q_refs[idx].at[head_idx], q_buf.at[slot, src, pl.ds(row0, rows)], sems.at[slot]))
        return out

    slot = lax.rem(head, 2)

    @pl.when(head == 0)
    def _():
        for cp in copies(0, 0):
            cp.start()

    @pl.when(head + 1 < n_heads)
    def _():
        for cp in copies(head + 1, 1 - slot):
            cp.start()

    for cp in copies(head, slot):
        cp.wait()

    row_i = lax.broadcasted_iota(jnp.int32, (PIECE, PIECE), 0)
    col_i = lax.broadcasted_iota(jnp.int32, (PIECE, PIECE), 1)

    for src in range(N_CP):
        q_piece = meta_ref[2 * N_CP + src]
        k_lo = meta_ref[3 * N_CP + q_piece]
        k_full = meta_ref[3 * N_CP + 2 * N_CP + q_piece]
        q0 = pl.multiple_of(q_piece * PIECE, PIECE)
        q_blk = q_buf[slot, src]
        starts = start_ref[pl.ds(q0, PIECE), :]

        def scores_of(k0):
            return lax.dot_general(q_blk, k_buf[slot, pl.ds(k0, PIECE), :], (((1,), (1,)), ((), ())), preferred_element_type=jnp.float32)

        def fold(p):
            total = p[:, :128]
            for lane in range(128, PIECE, 128):
                total = total + p[:, lane:lane + 128]
            return total

        s = scores_of(q0)
        s = jnp.where((col_i <= row_i) & (col_i >= starts - q0), s, NEG_BIG)
        m_new = jnp.max(s, axis=1, keepdims=True)
        p = jnp.exp2(s * coef - m_new * coef)
        m_ref[...] = jnp.broadcast_to(m_new, m_ref.shape)
        l_ref[...] = fold(p)
        acc_ref[...] = jnp.dot(p.astype(jnp.bfloat16), v_buf[slot, pl.ds(q0, PIECE), :], preferred_element_type=jnp.float32)

        def step(kb, masked):
            k0 = pl.multiple_of(kb * PIECE, PIECE)
            s = scores_of(k0)
            if masked:
                s = jnp.where(col_i >= starts - k0, s, NEG_BIG)
            m_old = m_ref[:, :1]
            m_new = jnp.maximum(m_old, jnp.max(s, axis=1, keepdims=True))
            alpha = jnp.exp2((m_old - m_new) * coef)
            p = jnp.exp2(s * coef - m_new * coef)
            m_ref[...] = jnp.broadcast_to(m_new, m_ref.shape)
            l_ref[...] = l_ref[...] * alpha + fold(p)
            acc_ref[...] = acc_ref[...] * alpha + jnp.dot(p.astype(jnp.bfloat16), v_buf[slot, pl.ds(k0, PIECE), :], preferred_element_type=jnp.float32)

        pl.loop(k_lo, k_full)(lambda kb: step(kb, True))
        pl.loop(k_full, q_piece)(lambda kb: step(kb, False))
        total = jnp.sum(l_ref[...], axis=1, keepdims=True)
        o_ref[src] = (acc_ref[...] / total).astype(jnp.bfloat16)


def attention(meta, starts, k_parts, v_parts, q_parts, chunk_rows, q_chunks, coef):
    n_heads, _, head_dim = k_parts[0].shape
    n_in = len(k_parts) + len(v_parts) + len(q_parts)
    seq = starts.shape[0]
    return pl.pallas_call(
        functools.partial(attn_kernel, n_heads=n_heads, chunk_rows=chunk_rows, q_chunks=q_chunks, coef=coef),
        grid_spec=pltpu.PrefetchScalarGridSpec(
            num_scalar_prefetch=1,
            grid=(n_heads,),
            in_specs=[pl.BlockSpec((seq, 1), lambda h, meta: (0, 0))] + [pl.BlockSpec(memory_space=pltpu.HBM)] * n_in,
            out_specs=pl.BlockSpec((N_CP, PIECE, head_dim), lambda h, meta: (0, 0, h)),
            scratch_shapes=[
                pltpu.VMEM((2, seq, head_dim), jnp.bfloat16),
                pltpu.VMEM((2, seq, head_dim), jnp.bfloat16),
                pltpu.VMEM((2, N_CP, PIECE, head_dim), jnp.bfloat16),
                pltpu.VMEM((PIECE, 128), jnp.float32),
                pltpu.VMEM((PIECE, 128), jnp.float32),
                pltpu.VMEM((PIECE, head_dim), jnp.float32),
                pltpu.SemaphoreType.DMA((2,)),
            ],
        ),
        out_shape=jax.ShapeDtypeStruct((N_CP, PIECE, n_heads * head_dim), jnp.bfloat16),
        compiler_params=pltpu.CompilerParams(dimension_semantics=("arbitrary",), vmem_limit_bytes=40 * 2**20),
        cost_estimate=pl.CostEstimate(flops=30 * 10**9, bytes_accessed=30 * 2**20, transcendentals=10**7),
        name="attention",
    )(meta, starts, *k_parts, *v_parts, *q_parts)


def out_kernel(group_ref, *refs, has_recv):
    o_refs, w_refs = refs[:N_CP], refs[N_CP:2 * N_CP]
    out_ref = refs[-1]
    total = jnp.dot(o_refs[0][...], w_refs[0][...], preferred_element_type=jnp.float32)
    for src in range(1, N_CP):
        total += jnp.dot(o_refs[src][...], w_refs[src][...], preferred_element_type=jnp.float32)
    if has_recv:
        total += refs[2 * N_CP][...]
    out_ref[...] = total.astype(out_ref.dtype)


def out_proj(groups, o_parts, w_out, col0, n_cols, recv=None, y_prev=None):
    rows, width = o_parts[0].shape
    blk = 512
    first = col0 // blk
    in_specs = [pl.BlockSpec((rows, width), lambda j, g: (0, 0))] * N_CP
    in_specs += [pl.BlockSpec((width, blk), functools.partial(lambda src, j, g: (g[src], first + j), src)) for src in range(N_CP)]
    args = list(o_parts) + [w_out] * N_CP
    aliases = {}
    if recv is None:
        out_shape = jax.ShapeDtypeStruct((rows, n_cols), jnp.float32)
        out_spec = pl.BlockSpec((rows, blk), lambda j, g: (0, j))
    else:
        in_specs.append(pl.BlockSpec((rows, blk), lambda j, g: (0, j)))
        args.append(recv)
        out_shape = jax.ShapeDtypeStruct((rows, w_out.shape[1]), jnp.bfloat16)
        out_spec = pl.BlockSpec((rows, blk), lambda j, g: (0, first + j))
        if y_prev is not None:
            aliases = {1 + len(args): 0}
            in_specs.append(pl.BlockSpec(memory_space=pl.ANY))
            args.append(y_prev)
    flops = 2 * rows * width * N_CP * n_cols
    return pl.pallas_call(
        functools.partial(out_kernel, has_recv=recv is not None),
        grid_spec=pltpu.PrefetchScalarGridSpec(
            num_scalar_prefetch=1, grid=(n_cols // blk,), in_specs=in_specs, out_specs=out_spec),
        out_shape=out_shape,
        input_output_aliases=aliases,
        compiler_params=pltpu.CompilerParams(dimension_semantics=("arbitrary",), vmem_limit_bytes=40 * 2**20),
        cost_estimate=pl.CostEstimate(flops=flops, bytes_accessed=2 * width * N_CP * n_cols + 4 * rows * n_cols, transcendentals=0),
        name="out_proj",
    )(groups, *args)


def solution(mesh):
    def per_device(x_loc, seg_loc, w_q, w_k, w_v, w_o):
        cp_rank = lax.axis_index("cp")
        tp_rank = lax.axis_index("tp")
        rows = x_loc.shape[0]
        n_loc, head_dim = w_k.shape[1:]
        n_grp = n_loc // N_CP
        coef = head_dim ** -0.5 * math.log2(math.e)
        half = rows // X_CHUNKS

        x_other = []
        for c in range(X_CHUNKS):
            x_other.append(lax.ppermute(x_loc[c * half:(c + 1) * half], "tp", SWAP))

        seg_all = lax.all_gather(seg_loc, ("cp", "tp"), axis=0, tiled=True).reshape(N_CP, 2, PIECE)
        seg_pos = jnp.concatenate([seg_all[:, 0], seg_all[::-1, 1]], axis=0).reshape(-1)
        seq = seg_pos.shape[0]
        n_blk = seq // PIECE
        starts = jnp.sum((seg_pos[None, :] < seg_pos[:, None]).astype(jnp.int32), axis=1)
        blk_starts = starts.reshape(n_blk, PIECE)
        k_lo = blk_starts[:, 0] // PIECE
        k_full = jnp.minimum((blk_starts[:, -1] + PIECE - 1) // PIECE, jnp.arange(n_blk))
        ranks = jnp.array([cp_rank ^ s for s in range(N_CP)])
        own_piece = jnp.where(tp_rank == 0, ranks, 2 * N_CP - 1 - ranks)
        other_piece = 2 * N_CP - 1 - own_piece

        def meta_of(q_piece):
            return jnp.concatenate([own_piece, other_piece, q_piece, k_lo, k_full]).astype(jnp.int32)

        def project(x_rows, w):
            out = jnp.einsum("sd,dhe->she", x_rows, w, preferred_element_type=jnp.float32).astype(jnp.bfloat16)
            return out.transpose(1, 0, 2)

        def slices(val):
            return [lax.dynamic_slice_in_dim(val, (cp_rank ^ s) * n_grp, n_grp, axis=0) for s in range(N_CP)]

        def exchange(parts):
            out = [parts[0]] + [None] * (N_CP - 1)
            for s in (2, 3, 1):
                out[s] = lax.ppermute(parts[s], "cp", [(d, d ^ s) for d in range(N_CP)])
            return out

        weights = (w_k, w_v, w_q)
        inputs = [x_loc] + x_other
        spread = []
        held = None
        for c, x_c in enumerate(inputs):
            done = []
            for i, w in enumerate(weights):
                if held is not None:
                    x_c, held = lax.optimization_barrier((x_c, held))
                    if c != 1 or i != 0:
                        (done if i else spread[-1]).append(exchange(held))
                val = project(x_c, w)
                held = slices(val)
                if c == 0 and i == 2:
                    q_own = held
            spread.append(done)
        spread[-1].append(exchange(held))
        ks, vs = [d[0] for d in spread], [d[1] for d in spread]
        qs = [d[2] for d in spread[1:]]

        chunk_rows = [(0, 0, rows)] + [(1, c * half, half) for c in range(X_CHUNKS)]
        k_parts = [ks[i][s] for s in range(N_CP) for i in range(1 + X_CHUNKS)]
        v_parts = [vs[i][s] for s in range(N_CP) for i in range(1 + X_CHUNKS)]
        starts_col = starts[:, None]
        o_other = attention(meta_of(other_piece), starts_col, k_parts, v_parts,
                            [qs[c][s] for s in range(N_CP) for c in range(X_CHUNKS)],
                            chunk_rows, [(c * half, half) for c in range(X_CHUNKS)], coef)

        w_out = w_o.reshape(n_loc * head_dim, -1)
        groups = ranks.astype(jnp.int32)
        back_other = exchange([o_other[s] for s in range(N_CP)])
        q_own, back_other = lax.optimization_barrier((q_own, back_other))
        qs_own = exchange(q_own)
        recvs = []
        part = None
        col0 = 0
        for n_cols in Y_SPLITS:
            if part is not None:
                groups, part = lax.optimization_barrier((groups, part))
                recvs.append(lax.ppermute(part, "tp", SWAP))
            part = out_proj(groups, back_other, w_out, col0, n_cols)
            col0 += n_cols
        meta_own, part = lax.optimization_barrier((meta_of(own_piece), part))
        recvs.append(lax.ppermute(part, "tp", SWAP))
        o_own = attention(meta_own, starts_col, k_parts, v_parts,
                          [qs_own[s] for s in range(N_CP)], chunk_rows, [(0, rows)], coef)
        back_own = exchange([o_own[s] for s in range(N_CP)])
        y = None
        col0 = 0
        for n_cols, recv in zip(Y_SPLITS, recvs):
            y = out_proj(groups, back_own, w_out, col0, n_cols, recv, y)
            col0 += n_cols
        return y

    return jax.shard_map(
        per_device,
        mesh=mesh,
        in_specs=(P(("dp", "cp", "tp"), None), P(("dp", "cp", "tp")), P(None, "tp", None), P(None, "tp", None), P(None, "tp", None), P("tp", None, None)),
        out_specs=P(("dp", "cp", "tp"), None),
        check_vma=False,
    )
```

time: 1980 us -> 1300 us (0.66)
  waiting for transfers between devices: 1100 us -> 327 us
  Pallas kernels: 0 us -> 395 us
  matrix products: 629 us -> 303 us
  starting transfers between devices: 1.75 us -> 158 us
  other arithmetic: 142 us -> 9.39 us
  blocking collectives: 5.66 us -> 56 us
  local copies, waits for them, and re-layouts: 73.8 us -> 43 us
    pallas_call x0 -> x20, Pallas kernels: none -> 395 us  [the longest x2 248 us: attention(): pl.pallas_call(functools.partial(attn_kernel, n_heads=n_heads, chunk_rows...]
    reduce_scatter x1 -> x0, waiting for transfers between devices: 365 us -> none  [per_device(): lax.psum_scatter(y_part, 'tp', scatter_dimension=0, tiled=True)]
    dot_general x12 -> x9, matrix products: 629 us -> 303 us  [project(): jnp.einsum('sd,dhe->she', x_rows, w, preferred_element_type=jnp.float32)]
    ppermute x9 -> x44, waiting for transfers between devices: 547 us -> 327 us  [the longest x9 218 us: per_device(): recvs.append(lax.ppermute(part, 'tp', SWAP))]
    all_gather x1 -> x0, waiting for transfers between devices: 192 us -> none  [per_device(): x_rows = lax.all_gather(x_loc, 'tp', axis=0, tiled=True)]
    ppermute x9 -> x44, starting transfers between devices: 1.71 us -> 158 us  [the longest x9 128 us: per_device(): recvs.append(lax.ppermute(part, 'tp', SWAP))]
    reduce_sum x4 -> x1, other arithmetic: 106 us -> 9.07 us  [per_device(): jnp.sum((seg_pos[None, :] < seg_pos[:, None]).astype(jnp.int32), axis=1)]
    all_gather x1, blocking collectives: 5.66 us -> 56 us  [per_device(): lax.all_gather(seg_loc, ('cp', 'tp'), axis=0, tiled=True)]
  transfers between devices with their start and end apart: 11 -> 44, of which waited for: 5 -> 16; matrix products, arithmetic and copies ran while one was open for 0% -> 23% of each run, Pallas kernels for 0% -> 17%
where the time goes in v1:
time: 1300 us; the launch traced here: 1290 us
  Pallas kernels  395 us (30%)
  waiting for transfers between devices  327 us (25%)
  matrix products  303 us (23%)
  starting transfers between devices  158 us (12%)
  blocking collectives  56 us (4%)
  local copies, waits for them, and re-layouts  43 us (3%)
    dot_general x9, matrix products, project(): jnp.einsum('sd,dhe->she', x_rows, w, preferred_element_type=jnp.float32)  303 us
    pallas_call x2, Pallas kernels, attention(): pl.pallas_call(functools.partial(attn_kernel, n_heads=n_heads, chunk_rows...  248 us
    ppermute x9, waiting for transfers between devices, per_device(): recvs.append(lax.ppermute(part, 'tp', SWAP))  218 us
    pallas_call x18, Pallas kernels, out_proj(): pl.pallas_call(functools.partial(out_kernel, has_recv=recv is not None),...  148 us
    ppermute x9, starting transfers between devices, per_device(): recvs.append(lax.ppermute(part, 'tp', SWAP))  128 us
    ppermute x33, waiting for transfers between devices, exchange(): out[s] = lax.ppermute(parts[s], 'cp', [(d, d ^ s) for d in range(N_CP)])  109 us
    all_gather x1, blocking collectives, per_device(): lax.all_gather(seg_loc, ('cp', 'tp'), axis=0, tiled=True)  56 us
    ppermute x33, starting transfers between devices, exchange(): out[s] = lax.ppermute(parts[s], 'cp', [(d, d ^ s) for d in range(N_CP)])  26.4 us
  transfers between devices with their start and end apart: 44, of which 16 were waited for; matrix products, arithmetic and copies ran while one was open for 23% of the time, Pallas kernels for 17%

profile of v1, /device:TPU:0, one launch (start us, length us, event | category | flops | bytes accessed | tf_op | source)
XLA Modules:
  0.0 1292.2 jit_solution(4115313591204059819)
XLA Ops:
  0.0 51.2 %fusion.27 = bf16[512,32,128]{2,0,1:T(8,128)(2,1)S(1)} fusion(bf16[8192,32,128]{2,1,0:T(8,128)(2,1)} %param.9, bf16[512,8192]{1,0:T(8,128)(2,1)} %param.6), kind=kOutput, calls=%fused_computation.28 | convolution fusion | flops 34361835520 | bytes 79691776 | tf_op jit(solution)/shard_map/sd,dhe->she/dot_general | solution.py:208
  56.4 40.6 %fusion.32 = bf16[512,32,128]{2,0,1:T(8,128)(2,1)S(1)} fusion(bf16[8192,32,128]{2,1,0:T(8,128)(2,1)} %param.10, bf16[512,8192]{1,0:T(8,128)(2,1)S(1)} %copy-done.18), kind=kOutput, calls=%fused_computation.29 | convolution fusion | flops 34361835520 | bytes 79691776 | tf_op jit(solution)/shard_map/sd,dhe->she/dot_general | solution.py:208
  105.9 42.0 %fusion.37 = bf16[512,32,128]{2,0,1:T(8,128)(2,1)} fusion(bf16[8192,32,128]{2,1,0:T(8,128)(2,1)} %param.8, bf16[512,8192]{1,0:T(8,128)(2,1)S(1)} %copy-done.18), kind=kOutput, calls=%fused_computation.30 | convolution fusion | flops 34361835520 | bytes 79691776 | tf_op jit(solution)/shard_map/sd,dhe->she/dot_general | solution.py:208
  147.9 56.0 %all-gather = s32[8,1,512]{2,1,0:T(1,128)S(1)} all-gather(s32[1,1,512]{2,1,0:T(1,128)S(1)} %bitcast.153), channel_id=1, replica_groups=mesh['dp'=1,'tp'=2,'cp'=4] {'cp','tp'}, dimensions={0}, use_global_device_ids=true | all-gather | bytes 18432 | tf_op jit(solution)/shard_map/all_gather | solution.py:192
  209.3 28.0 %fusion.42 = bf16[256,32,128]{2,0,1:T(8,128)(2,1)} fusion(bf16[8192,32,128]{2,1,0:T(8,128)(2,1)} %param.9, bf16[256,8192]{1,0:T(8,128)(2,1)} %collective-permute-done), kind=kOutput, calls=%fused_computation.31 | convolution fusion | flops 17180917760 | bytes 73400320 | tf_op jit(solution)/shard_map/sd,dhe->she/dot_general | solution.py:208
  240.1 28.2 %fusion.52 = bf16[256,32,128]{2,0,1:T(8,128)(2,1)} fusion(bf16[8192,32,128]{2,1,0:T(8,128)(2,1)} %param.10, bf16[256,8192]{1,0:T(8,128)(2,1)} %collective-permute-done), kind=kOutput, calls=%fused_computation.33 | convolution fusion | flops 17180917760 | bytes 73400320 | tf_op jit(solution)/shard_map/sd,dhe->she/dot_general | solution.py:208
  271.0 28.2 %fusion.62 = bf16[256,32,128]{2,0,1:T(8,128)(2,1)} fusion(bf16[8192,32,128]{2,1,0:T(8,128)(2,1)} %param.8, bf16[256,8192]{1,0:T(8,128)(2,1)} %collective-permute-done), kind=kOutput, calls=%fused_computation.35 | convolution fusion | flops 17180917760 | bytes 73400320 | tf_op jit(solution)/shard_map/sd,dhe->she/dot_general | solution.py:208
  305.7 28.0 %fusion.47 = bf16[256,32,128]{2,0,1:T(8,128)(2,1)} fusion(bf16[8192,32,128]{2,1,0:T(8,128)(2,1)} %param.9, bf16[256,8192]{1,0:T(8,128)(2,1)} %collective-permute-done.1), kind=kOutput, calls=%fused_computation.32 | convolution fusion | flops 17180917760 | bytes 73400320 | tf_op jit(solution)/shard_map/sd,dhe->she/dot_general | solution.py:208
  373.0 28.2 %fusion.57 = bf16[256,32,128]{2,0,1:T(8,128)(2,1)} fusion(bf16[8192,32,128]{2,1,0:T(8,128)(2,1)} %param.10, bf16[256,8192]{1,0:T(8,128)(2,1)} %collective-permute-done.1), kind=kOutput, calls=%fused_computation.34 | convolution fusion | flops 17180917760 | bytes 73400320 | tf_op jit(solution)/shard_map/sd,dhe->she/dot_general | solution.py:208
  407.8 28.0 %fusion.67 = bf16[256,32,128]{2,0,1:T(8,128)(2,1)} fusion(bf16[8192,32,128]{2,1,0:T(8,128)(2,1)} %param.8, bf16[256,8192]{1,0:T(8,128)(2,1)} %collective-permute-done.1), kind=kOutput, calls=%fused_computation.36 | convolution fusion | flops 17180917760 | bytes 73400320 | tf_op jit(solution)/shard_map/sd,dhe->she/dot_general | solution.py:208
  489.9 161.5 %attention.2 = bf16[4,512,1024]{2,1,0:T(8,128)(2,1)} custom-call(s32[28]{0:T(128)S(1)} %concatenate.14.meta_ref, s32[4096,1]{1,0:T(8,128)} %copy.71.start_ref, bf16[8,512,128]{2,1,0:T(8,128)(2,1)S(1)} %get-tuple-element.69.refs_0_, bf16[8,256,128]{2,1,0:T(8,128)(2,1)S(1)} %get-tuple-element.71.refs_1_, bf16[8,256,128]{2,1,0:T(8,128)(2,1)S(1)} %get-tuple-element.75.refs_2_, ...), custom_call_target="tpu_custom_call" | custom-call | flops 30000001024 | bytes 31457280 | tf_op jit(solution)/shard_map/attention/pallas_call | solution.py:110
  657.2 23.7 %collective-permute-done.28.refs_3_ = bf16[512,1024]{1,0:T(8,128)(2,1)S(1)} collective-permute-done((bf16[512,1024]{1,0:T(8,128)(2,1)}, bf16[512,1024]{1,0:T(8,128)(2,1)S(1)}, u32[]{:S(2)}, u32[]{:S(2)}) %collective-permute-start.28) | collective-permute-done | bytes 1048608 | tf_op jit(solution)/shard_map/ppermute | solution.py:217
  680.9 21.5 %collective-permute-done.27.refs_2_ = bf16[512,1024]{1,0:T(8,128)(2,1)S(1)} collective-permute-done((bf16[512,1024]{1,0:T(8,128)(2,1)}, bf16[512,1024]{1,0:T(8,128)(2,1)S(1)}, u32[]{:S(2)}, u32[]{:S(2)}) %collective-permute-start.27) | collective-permute-done | bytes 1048608 | tf_op jit(solution)/shard_map/ppermute | solution.py:217
  779.9 86.2 %attention.3 = bf16[4,512,1024]{2,1,0:T(8,128)(2,1)} custom-call(s32[28]{0:T(128)S(1)} %concatenate.15.meta_ref, s32[4096,1]{1,0:T(8,128)} %copy.71.start_ref, bf16[8,512,128]{2,1,0:T(8,128)(2,1)S(1)} %copy-done.3, bf16[8,256,128]{2,1,0:T(8,128)(2,1)S(1)} %copy-done.6, bf16[8,256,128]{2,1,0:T(8,128)(2,1)S(1)} %copy-done.10, ...), custom_call_target="tpu_custom_call" | custom-call | flops 30000001024 | bytes 31457280 | tf_op jit(solution)/shard_map/attention/pallas_call | solution.py:110
  869.9 77.3 %collective-permute-start.41 = (f32[512,1024]{1,0:T(8,128)S(1)}, f32[512,1024]{1,0:T(8,128)S(1)}, u32[]{:S(2)}, u32[]{:S(2)}) collective-permute-start(f32[512,1024]{1,0:T(8,128)S(1)} %out_proj.20), channel_id=1, source_target_pairs={{0,4},{4,0},{1,5},{5,1},{2,6},{6,2},{3,7},{7,3}} | collective-permute-start | bytes 6291464 | tf_op jit(solution)/shard_map/ppermute | solution.py:259
  947.8 23.3 %collective-permute-start.40 = (f32[512,1024]{1,0:T(8,128)}, f32[512,1024]{1,0:T(8,128)}, u32[]{:S(2)}, u32[]{:S(2)}) collective-permute-start(f32[512,1024]{1,0:T(8,128)} %out_proj.21), channel_id=1, source_target_pairs={{0,4},{4,0},{1,5},{5,1},{2,6},{6,2},{3,7},{7,3}} | collective-permute-start | bytes 6291464 | tf_op jit(solution)/shard_map/ppermute | solution.py:259
  972.3 21.6 %collective-permute-start.39 = (f32[512,1024]{1,0:T(8,128)}, f32[512,1024]{1,0:T(8,128)}, u32[]{:S(2)}, u32[]{:S(2)}) collective-permute-start(f32[512,1024]{1,0:T(8,128)} %out_proj.22), channel_id=1, source_target_pairs={{0,4},{4,0},{1,5},{5,1},{2,6},{6,2},{3,7},{7,3}} | collective-permute-start | bytes 6291464 | tf_op jit(solution)/shard_map/ppermute | solution.py:259
  1003.5 35.2 %collective-permute-done.42.refs_8_ = f32[512,1024]{1,0:T(8,128)S(1)} collective-permute-done((f32[512,1024]{1,0:T(8,128)S(1)}, f32[512,1024]{1,0:T(8,128)S(1)}, u32[]{:S(2)}, u32[]{:S(2)}) %collective-permute-start.42) | collective-permute-done | bytes 2097184 | tf_op jit(solution)/shard_map/ppermute | solution.py:259
  1057.5 26.2 %collective-permute-done.40.refs_8_ = f32[512,1024]{1,0:T(8,128)} collective-permute-done((f32[512,1024]{1,0:T(8,128)}, f32[512,1024]{1,0:T(8,128)}, u32[]{:S(2)}, u32[]{:S(2)}) %collective-permute-start.40) | collective-permute-done | bytes 2097184 | tf_op jit(solution)/shard_map/ppermute | solution.py:259
  1094.4 34.3 %collective-permute-done.39.refs_8_ = f32[512,1024]{1,0:T(8,128)} collective-permute-done((f32[512,1024]{1,0:T(8,128)}, f32[512,1024]{1,0:T(8,128)}, u32[]{:S(2)}, u32[]{:S(2)}) %collective-permute-start.39) | collective-permute-done | bytes 2097184 | tf_op jit(solution)/shard_map/ppermute | solution.py:259
  1137.3 36.3 %collective-permute-done.38.refs_8_ = f32[512,1024]{1,0:T(8,128)} collective-permute-done((f32[512,1024]{1,0:T(8,128)}, f32[512,1024]{1,0:T(8,128)}, u32[]{:S(2)}, u32[]{:S(2)}) %collective-permute-start.38) | collective-permute-done | bytes 2097184 | tf_op jit(solution)/shard_map/ppermute | solution.py:259
  1182.2 36.3 %collective-permute-done.37.refs_8_ = f32[512,1024]{1,0:T(8,128)} collective-permute-done((f32[512,1024]{1,0:T(8,128)}, f32[512,1024]{1,0:T(8,128)}, u32[]{:S(2)}, u32[]{:S(2)}) %collective-permute-start.37) | collective-permute-done | bytes 2097184 | tf_op jit(solution)/shard_map/ppermute | solution.py:259
  1227.2 36.3 %collective-permute-done.36.refs_8_ = f32[512,1024]{1,0:T(8,128)} collective-permute-done((f32[512,1024]{1,0:T(8,128)}, f32[512,1024]{1,0:T(8,128)}, u32[]{:S(2)}, u32[]{:S(2)}) %collective-permute-start.36) | collective-permute-done | bytes 2097184 | tf_op jit(solution)/shard_map/ppermute | solution.py:259
  1272.1 13.5 %collective-permute-done.35.refs_8_ = f32[512,512]{1,0:T(8,128)} collective-permute-done((f32[512,512]{1,0:T(8,128)}, f32[512,512]{1,0:T(8,128)}, u32[]{:S(2)}, u32[]{:S(2)}) %collective-permute-start.35) | collective-permute-done | bytes 1048608 | tf_op jit(solution)/shard_map/ppermute | solution.py:263
  (164 shorter events, 299.6 us)
Async XLA Ops:
  53.0 249.5 %collective-permute-start.2 = (bf16[8,512,128]{2,1,0:T(8,128)(2,1)}, bf16[8,512,128]{2,1,0:T(8,128)(2,1)}, u32[]{:S(2)}, u32[]{:S(2)}) collective-permute-start(bf16[8,512,128]{2,1,0:T(8,128)(2,1)} %get-tuple-element.76), channel_id=1, source_target_pairs={{0,1},{1,0},{2,3},{3,2},{4,5},{5,4},{6,7},{7,6}} | collective-permute-start | bytes 3145736 | tf_op jit(solution)/shard_map/ppermute | solution.py:217
  53.8 248.6 %collective-permute-start.5 = (bf16[8,512,128]{2,1,0:T(8,128)(2,1)}, bf16[8,512,128]{2,1,0:T(8,128)(2,1)}, u32[]{:S(2)}, u32[]{:S(2)}) collective-permute-start(bf16[8,512,128]{2,1,0:T(8,128)(2,1)} %get-tuple-element.79), channel_id=1, source_target_pairs={{0,2},{1,3},{2,0},{3,1},{4,6},{5,7},{6,4},{7,5}} | collective-permute-start | bytes 3145736 | tf_op jit(solution)/shard_map/ppermute | solution.py:217
  56.3 248.0 %collective-permute-start.8 = (bf16[8,512,128]{2,1,0:T(8,128)(2,1)}, bf16[8,512,128]{2,1,0:T(8,128)(2,1)}, u32[]{:S(2)}, u32[]{:S(2)}) collective-permute-start(bf16[8,512,128]{2,1,0:T(8,128)(2,1)} %get-tuple-element.82), channel_id=1, source_target_pairs={{0,3},{1,2},{2,1},{3,0},{4,7},{5,6},{6,5},{7,4}} | collective-permute-start | bytes 3145736 | tf_op jit(solution)/shard_map/ppermute | solution.py:217
  99.0 205.6 %collective-permute-start.11 = (bf16[8,512,128]{2,1,0:T(8,128)(2,1)}, bf16[8,512,128]{2,1,0:T(8,128)(2,1)}, u32[]{:S(2)}, u32[]{:S(2)}) collective-permute-start(bf16[8,512,128]{2,1,0:T(8,128)(2,1)} %get-tuple-element.89), channel_id=1, source_target_pairs={{0,1},{1,0},{2,3},{3,2},{4,5},{5,4},{6,7},{7,6}} | collective-permute-start | bytes 3145736 | tf_op jit(solution)/shard_map/ppermute | solution.py:217
  103.4 105.5 %collective-permute-start = (bf16[256,8192]{1,0:T(8,128)(2,1)}, bf16[256,8192]{1,0:T(8,128)(2,1)}, u32[]{:S(2)}, u32[]{:S(2)}) collective-permute-start(bf16[256,8192]{1,0:T(8,128)(2,1)} %get-tuple-element.135), channel_id=1, source_target_pairs={{0,4},{4,0},{1,5},{5,1},{2,6},{6,2},{3,7},{7,3}} | collective-permute-start | bytes 12582920 | tf_op jit(solution)/shard_map/ppermute | solution.py:190
  208.8 93.3 %collective-permute-start.1 = (bf16[256,8192]{1,0:T(8,128)(2,1)}, bf16[256,8192]{1,0:T(8,128)(2,1)}, u32[]{:S(2)}, u32[]{:S(2)}) collective-permute-start(bf16[256,8192]{1,0:T(8,128)(2,1)} %get-tuple-element.134), channel_id=1, source_target_pairs={{0,4},{4,0},{1,5},{5,1},{2,6},{6,2},{3,7},{7,3}} | collective-permute-start | bytes 12582920 | tf_op jit(solution)/shard_map/ppermute | solution.py:190
  304.3 57.9 %collective-permute-start.6 = (bf16[8,256,128]{2,1,0:T(8,128)(2,1)}, bf16[8,256,128]{2,1,0:T(8,128)(2,1)}, u32[]{:S(2)}, u32[]{:S(2)}) collective-permute-start(bf16[8,256,128]{2,1,0:T(8,128)(2,1)} %get-tuple-element.80), channel_id=1, source_target_pairs={{0,2},{1,3},{2,0},{3,1},{4,6},{5,7},{6,4},{7,5}} | collective-permute-start | bytes 1572872 | tf_op jit(solution)/shard_map/ppermute | solution.py:217
  304.6 66.6 %collective-permute-start.9 = (bf16[8,256,128]{2,1,0:T(8,128)(2,1)}, bf16[8,256,128]{2,1,0:T(8,128)(2,1)}, u32[]{:S(2)}, u32[]{:S(2)}) collective-permute-start(bf16[8,256,128]{2,1,0:T(8,128)(2,1)} %get-tuple-element.83), channel_id=1, source_target_pairs={{0,3},{1,2},{2,1},{3,0},{4,7},{5,6},{6,5},{7,4}} | collective-permute-start | bytes 1572872 | tf_op jit(solution)/shard_map/ppermute | solution.py:217
  336.5 67.5 %collective-permute-start.20 = (bf16[8,256,128]{2,1,0:T(8,128)(2,1)}, bf16[8,256,128]{2,1,0:T(8,128)(2,1)}, u32[]{:S(2)}, u32[]{:S(2)}) collective-permute-start(bf16[8,256,128]{2,1,0:T(8,128)(2,1)} %get-tuple-element.100), channel_id=1, source_target_pairs={{0,1},{1,0},{2,3},{3,2},{4,5},{5,4},{6,7},{7,6}} | collective-permute-start | bytes 1572872 | tf_op jit(solution)/shard_map/ppermute | solution.py:217
  348.8 56.8 %collective-permute-start.22 = (bf16[8,256,128]{2,1,0:T(8,128)(2,1)}, bf16[8,256,128]{2,1,0:T(8,128)(2,1)}, u32[]{:S(2)}, u32[]{:S(2)}) collective-permute-start(bf16[8,256,128]{2,1,0:T(8,128)(2,1)} %get-tuple-element.101), channel_id=1, source_target_pairs={{0,2},{1,3},{2,0},{3,1},{4,6},{5,7},{6,4},{7,5}} | collective-permute-start | bytes 1572872 | tf_op jit(solution)/shard_map/ppermute | solution.py:217
  351.3 54.3 %collective-permute-start.24 = (bf16[8,256,128]{2,1,0:T(8,128)(2,1)}, bf16[8,256,128]{2,1,0:T(8,128)(2,1)}, u32[]{:S(2)}, u32[]{:S(2)}) collective-permute-start(bf16[8,256,128]{2,1,0:T(8,128)(2,1)} %get-tuple-element.102), channel_id=1, source_target_pairs={{0,3},{1,2},{2,1},{3,0},{4,7},{5,6},{6,5},{7,4}} | collective-permute-start | bytes 1572872 | tf_op jit(solution)/shard_map/ppermute | solution.py:217
  708.8 239.0 %collective-permute-start.43 = (f32[512,512]{1,0:T(8,128)}, f32[512,512]{1,0:T(8,128)}, u32[]{:S(2)}, u32[]{:S(2)}) collective-permute-start(f32[512,512]{1,0:T(8,128)} %out_proj.18), channel_id=1, source_target_pairs={{0,4},{4,0},{1,5},{5,1},{2,6},{6,2},{3,7},{7,3}} | collective-permute-start | bytes 3145736 | tf_op jit(solution)/shard_map/ppermute | solution.py:259
  708.8 71.0 %collective-permute-start.29 = (bf16[8,512,128]{2,1,0:T(8,128)(2,1)}, bf16[8,512,128]{2,1,0:T(8,128)(2,1)}, u32[]{:S(2)}, u32[]{:S(2)}) collective-permute-start(bf16[8,512,128]{2,1,0:T(8,128)(2,1)} %get-tuple-element.117), channel_id=1, source_target_pairs={{0,1},{1,0},{2,3},{3,2},{4,5},{5,4},{6,7},{7,6}} | collective-permute-start | bytes 3145736 | tf_op jit(solution)/shard_map/ppermute | solution.py:217
  709.1 70.7 %collective-permute-start.30 = (bf16[8,512,128]{2,1,0:T(8,128)(2,1)}, bf16[8,512,128]{2,1,0:T(8,128)(2,1)}, u32[]{:S(2)}, u32[]{:S(2)}) collective-permute-start(bf16[8,512,128]{2,1,0:T(8,128)(2,1)} %get-tuple-element.118), channel_id=1, source_target_pairs={{0,2},{1,3},{2,0},{3,1},{4,6},{5,7},{6,4},{7,5}} | collective-permute-start | bytes 3145736 | tf_op jit(solution)/shard_map/ppermute | solution.py:217
  710.2 69.7 %collective-permute-start.31 = (bf16[8,512,128]{2,1,0:T(8,128)(2,1)}, bf16[8,512,128]{2,1,0:T(8,128)(2,1)}, u32[]{:S(2)}, u32[]{:S(2)}) collective-permute-start(bf16[8,512,128]{2,1,0:T(8,128)(2,1)} %get-tuple-element.119), channel_id=1, source_target_pairs={{0,3},{1,2},{2,1},{3,0},{4,7},{5,6},{6,5},{7,4}} | collective-permute-start | bytes 3145736 | tf_op jit(solution)/shard_map/ppermute | solution.py:217
  868.7 79.1 %collective-permute-start.34 = (bf16[512,1024]{1,0:T(8,128)(2,1)S(1)}, bf16[512,1024]{1,0:T(8,128)(2,1)S(1)}, u32[]{:S(2)}, u32[]{:S(2)}) collective-permute-start(bf16[512,1024]{1,0:T(8,128)(2,1)S(1)} %get-tuple-element.136), channel_id=1, source_target_pairs={{0,3},{1,2},{2,1},{3,0},{4,7},{5,6},{6,5},{7,4}} | collective-permute-start | bytes 3145736 | tf_op jit(solution)/shard_map/ppermute | solution.py:217
  869.9 124.0 %collective-permute-start.41 = (f32[512,1024]{1,0:T(8,128)S(1)}, f32[512,1024]{1,0:T(8,128)S(1)}, u32[]{:S(2)}, u32[]{:S(2)}) collective-permute-start(f32[512,1024]{1,0:T(8,128)S(1)} %out_proj.20), channel_id=1, source_target_pairs={{0,4},{4,0},{1,5},{5,1},{2,6},{6,2},{3,7},{7,3}} | collective-permute-start | bytes 6291464 | tf_op jit(solution)/shard_map/ppermute | solution.py:259
  947.2 91.4 %collective-permute-start.42 = (f32[512,1024]{1,0:T(8,128)S(1)}, f32[512,1024]{1,0:T(8,128)S(1)}, u32[]{:S(2)}, u32[]{:S(2)}) collective-permute-start(f32[512,1024]{1,0:T(8,128)S(1)} %out_proj.19), channel_id=1, source_target_pairs={{0,4},{4,0},{1,5},{5,1},{2,6},{6,2},{3,7},{7,3}} | collective-permute-start | bytes 6291464 | tf_op jit(solution)/shard_map/ppermute | solution.py:259
  947.8 135.9 %collective-permute-start.40 = (f32[512,1024]{1,0:T(8,128)}, f32[512,1024]{1,0:T(8,128)}, u32[]{:S(2)}, u32[]{:S(2)}) collective-permute-start(f32[512,1024]{1,0:T(8,128)} %out_proj.21), channel_id=1, source_target_pairs={{0,4},{4,0},{1,5},{5,1},{2,6},{6,2},{3,7},{7,3}} | collective-permute-start | bytes 6291464 | tf_op jit(solution)/shard_map/ppermute | solution.py:259
  972.3 156.3 %collective-permute-start.39 = (f32[512,1024]{1,0:T(8,128)}, f32[512,1024]{1,0:T(8,128)}, u32[]{:S(2)}, u32[]{:S(2)}) collective-permute-start(f32[512,1024]{1,0:T(8,128)} %out_proj.22), channel_id=1, source_target_pairs={{0,4},{4,0},{1,5},{5,1},{2,6},{6,2},{3,7},{7,3}} | collective-permute-start | bytes 6291464 | tf_op jit(solution)/shard_map/ppermute | solution.py:259
  993.9 179.7 %collective-permute-start.38 = (f32[512,1024]{1,0:T(8,128)}, f32[512,1024]{1,0:T(8,128)}, u32[]{:S(2)}, u32[]{:S(2)}) collective-permute-start(f32[512,1024]{1,0:T(8,128)} %out_proj.23), channel_id=1, source_target_pairs={{0,4},{4,0},{1,5},{5,1},{2,6},{6,2},{3,7},{7,3}} | collective-permute-start | bytes 6291464 | tf_op jit(solution)/shard_map/ppermute | solution.py:259
  995.3 223.2 %collective-permute-start.37 = (f32[512,1024]{1,0:T(8,128)}, f32[512,1024]{1,0:T(8,128)}, u32[]{:S(2)}, u32[]{:S(2)}) collective-permute-start(f32[512,1024]{1,0:T(8,128)} %out_proj.24), channel_id=1, source_target_pairs={{0,4},{4,0},{1,5},{5,1},{2,6},{6,2},{3,7},{7,3}} | collective-permute-start | bytes 6291464 | tf_op jit(solution)/shard_map/ppermute | solution.py:259
  1038.7 224.8 %collective-permute-start.36 = (f32[512,1024]{1,0:T(8,128)}, f32[512,1024]{1,0:T(8,128)}, u32[]{:S(2)}, u32[]{:S(2)}) collective-permute-start(f32[512,1024]{1,0:T(8,128)} %out_proj.25), channel_id=1, source_target_pairs={{0,4},{4,0},{1,5},{5,1},{2,6},{6,2},{3,7},{7,3}} | collective-permute-start | bytes 6291464 | tf_op jit(solution)/shard_map/ppermute | solution.py:259
  1083.7 201.8 %collective-permute-start.35 = (f32[512,512]{1,0:T(8,128)}, f32[512,512]{1,0:T(8,128)}, u32[]{:S(2)}, u32[]{:S(2)}) collective-permute-start(f32[512,512]{1,0:T(8,128)} %out_proj.26), channel_id=1, source_target_pairs={{0,4},{4,0},{1,5},{5,1},{2,6},{6,2},{3,7},{7,3}} | collective-permute-start | bytes 3145736 | tf_op jit(solution)/shard_map/ppermute | solution.py:263
  (41 other events, 2019.3 us)

commit v2 on v1

v2 whole, which is shorter than its diff:
```python
import functools
import math

import jax
import jax.numpy as jnp
from jax import lax
from jax.experimental import pallas as pl
from jax.experimental.pallas import tpu as pltpu
from jax.sharding import PartitionSpec as P


NEG_BIG = -1e30
N_CP = 4
PIECE = 512
PAIR = 2
HALVES = 2
X_CHUNKS = 2
Y_SPLITS = (512, 1024, 1024, 1024, 1024, 1024, 1024, 1024, 512)
SWAP = [(0, 1), (1, 0)]


def attn_kernel(meta_ref, start_ref, *refs, head0, n_steps, k_chunks, q_chunks, coef):
    n_parts = len(k_chunks)
    n_k = N_CP * n_parts
    n_q = N_CP * len(q_chunks)
    k_refs, v_refs = refs[:n_k], refs[n_k:2 * n_k]
    q_refs = refs[2 * n_k:2 * n_k + n_q]
    o_ref = refs[2 * n_k + n_q]
    k_buf, v_buf, q_buf, acc_ref, sems = refs[2 * n_k + n_q + 1:]
    step_idx = pl.program_id(0)

    def copies(idx, slot):
        heads = pl.ds(head0 + idx * PAIR, PAIR)
        out = []
        for src in range(N_CP):
            for part, (kind, row0, rows) in enumerate(k_chunks):
                piece = meta_ref[kind * N_CP + src]
                dst = pl.ds(pl.multiple_of(piece * PIECE + row0, 128), rows)
                i = src * n_parts + part
                out.append(pltpu.make_async_copy(k_refs[i].at[heads], k_buf.at[slot, :, dst], sems.at[slot]))
                out.append(pltpu.make_async_copy(v_refs[i].at[heads], v_buf.at[slot, :, dst], sems.at[slot]))
            for part, (row0, rows) in enumerate(q_chunks):
                i = src * len(q_chunks) + part
                out.append(pltpu.make_async_copy(q_refs[i].at[heads], q_buf.at[slot, :, src, pl.ds(row0, rows)], sems.at[slot]))
        return out

    slot = lax.rem(step_idx, 2)

    @pl.when(step_idx == 0)
    def _():
        for cp in copies(0, 0):
            cp.start()

    @pl.when(step_idx + 1 < n_steps)
    def _():
        for cp in copies(step_idx + 1, 1 - slot):
            cp.start()

    for cp in copies(step_idx, slot):
        cp.wait()

    key_i = lax.broadcasted_iota(jnp.int32, (PIECE, PIECE), 0)
    qry_i = lax.broadcasted_iota(jnp.int32, (PIECE, PIECE), 1)

    for src in range(N_CP):
        q_piece = meta_ref[2 * N_CP + src]
        k_lo = meta_ref[3 * N_CP + src]
        k_full = meta_ref[4 * N_CP + src]
        q0 = pl.multiple_of(q_piece * PIECE, PIECE)
        starts = start_ref[src]

        def scores_of(h, k0):
            return lax.dot_general(k_buf[slot, h, pl.ds(k0, PIECE), :], q_buf[slot, h, src], (((1,), (1,)), ((), ())), preferred_element_type=jnp.float32)

        def weighted(h, k0, p):
            return lax.dot_general(v_buf[slot, h, pl.ds(k0, PIECE), :], p.astype(jnp.bfloat16), (((0,), (0,)), ((), ())), preferred_element_type=jnp.float32)

        state = []
        for h in range(PAIR):
            s = scores_of(h, q0)
            s = jnp.where((key_i <= qry_i) & (key_i >= starts - q0), s, NEG_BIG)
            m_new = jnp.max(s, axis=0, keepdims=True)
            p = jnp.exp2(s * coef - m_new * coef)
            acc_ref[h] = weighted(h, q0, p)
            state.append((m_new, jnp.sum(p, axis=0, keepdims=True)))

        def step(kb, state, masked):
            k0 = pl.multiple_of(kb * PIECE, PIECE)
            out = []
            for h in range(PAIR):
                m_old, l_old = state[h]
                s = scores_of(h, k0)
                if masked:
                    s = jnp.where(key_i >= starts - k0, s, NEG_BIG)
                m_new = jnp.maximum(m_old, jnp.max(s, axis=0, keepdims=True))
                alpha = jnp.exp2((m_old - m_new) * coef)
                p = jnp.exp2(s * coef - m_new * coef)
                acc_ref[h] = acc_ref[h] * alpha + weighted(h, k0, p)
                out.append((m_new, l_old * alpha + jnp.sum(p, axis=0, keepdims=True)))
            return tuple(out)

        state = lax.fori_loop(k_lo, k_full, functools.partial(step, masked=True), tuple(state))
        state = lax.fori_loop(k_full, q_piece, functools.partial(step, masked=False), state)
        for h in range(PAIR):
            out = acc_ref[h] / state[h][1]
            o_ref[src, :, h * 128:(h + 1) * 128] = out.T.astype(jnp.bfloat16)


def attention(meta, starts, k_parts, v_parts, q_parts, k_chunks, q_chunks, coef, head0, n_heads):
    head_dim = k_parts[0].shape[-1]
    n_in = len(k_parts) + len(v_parts) + len(q_parts)
    seq = 2 * N_CP * PIECE
    n_steps = n_heads // PAIR
    return pl.pallas_call(
        functools.partial(attn_kernel, head0=head0, n_steps=n_steps, k_chunks=k_chunks, q_chunks=q_chunks, coef=coef),
        grid_spec=pltpu.PrefetchScalarGridSpec(
            num_scalar_prefetch=1,
            grid=(n_steps,),
            in_specs=[pl.BlockSpec((N_CP, 1, PIECE), lambda h, meta: (0, 0, 0))] + [pl.BlockSpec(memory_space=pltpu.HBM)] * n_in,
            out_specs=pl.BlockSpec((N_CP, PIECE, PAIR * head_dim), lambda h, meta: (0, 0, h)),
            scratch_shapes=[
                pltpu.VMEM((2, PAIR, seq, head_dim), jnp.bfloat16),
                pltpu.VMEM((2, PAIR, seq, head_dim), jnp.bfloat16),
                pltpu.VMEM((2, PAIR, N_CP, PIECE, head_dim), jnp.bfloat16),
                pltpu.VMEM((PAIR, head_dim, PIECE), jnp.float32),
                pltpu.SemaphoreType.DMA((2,)),
            ],
        ),
        out_shape=jax.ShapeDtypeStruct((N_CP, PIECE, n_heads * head_dim), jnp.bfloat16),
        compiler_params=pltpu.CompilerParams(dimension_semantics=("arbitrary",), vmem_limit_bytes=48 * 2**20),
        cost_estimate=pl.CostEstimate(flops=15 * 10**9, bytes_accessed=15 * 2**20, transcendentals=10**7),
        name="attention",
    )(meta, starts, *k_parts, *v_parts, *q_parts)


def out_kernel(group_ref, *refs, n_parts, has_recv):
    o_refs, w_refs = refs[:n_parts], refs[n_parts:2 * n_parts]
    out_ref = refs[-1]
    total = jnp.dot(o_refs[0][...], w_refs[0][...], preferred_element_type=jnp.float32)
    for src in range(1, n_parts):
        total += jnp.dot(o_refs[src][...], w_refs[src][...], preferred_element_type=jnp.float32)
    if has_recv:
        total += refs[2 * n_parts][...]
    out_ref[...] = total.astype(out_ref.dtype)


def out_proj(groups, o_parts, w_out, col0, n_cols, recv=None, y_prev=None):
    rows, width = o_parts[0].shape
    n_parts = len(o_parts)
    blk = 512
    first = col0 // blk
    in_specs = [pl.BlockSpec((rows, width), lambda j, g: (0, 0))] * n_parts
    in_specs += [pl.BlockSpec((width, blk), functools.partial(lambda src, j, g: (g[src], first + j), src)) for src in range(n_parts)]
    args = list(o_parts) + [w_out] * n_parts
    aliases = {}
    if recv is None:
        out_shape = jax.ShapeDtypeStruct((rows, n_cols), jnp.float32)
        out_spec = pl.BlockSpec((rows, blk), lambda j, g: (0, j))
    else:
        in_specs.append(pl.BlockSpec((rows, blk), lambda j, g: (0, j)))
        args.append(recv)
        out_shape = jax.ShapeDtypeStruct((rows, w_out.shape[1]), jnp.bfloat16)
        out_spec = pl.BlockSpec((rows, blk), lambda j, g: (0, first + j))
        if y_prev is not None:
            aliases = {1 + len(args): 0}
            in_specs.append(pl.BlockSpec(memory_space=pl.ANY))
            args.append(y_prev)
    flops = 2 * rows * width * n_parts * n_cols
    return pl.pallas_call(
        functools.partial(out_kernel, n_parts=n_parts, has_recv=recv is not None),
        grid_spec=pltpu.PrefetchScalarGridSpec(
            num_scalar_prefetch=1, grid=(n_cols // blk,), in_specs=in_specs, out_specs=out_spec),
        out_shape=out_shape,
        input_output_aliases=aliases,
        compiler_params=pltpu.CompilerParams(dimension_semantics=("arbitrary",), vmem_limit_bytes=40 * 2**20),
        cost_estimate=pl.CostEstimate(flops=flops, bytes_accessed=2 * width * n_parts * n_cols + 4 * rows * n_cols, transcendentals=0),
        name="out_proj",
    )(groups, *args)


def solution(mesh):
    def per_device(x_loc, seg_loc, w_q, w_k, w_v, w_o):
        cp_rank = lax.axis_index("cp")
        tp_rank = lax.axis_index("tp")
        rows = x_loc.shape[0]
        n_loc, head_dim = w_k.shape[1:]
        n_grp = n_loc // N_CP
        coef = head_dim ** -0.5 * math.log2(math.e)
        half = rows // X_CHUNKS

        def cp_perm(s):
            return [(d, d ^ s) for d in range(N_CP)]

        seg_pair = jnp.stack([seg_loc, lax.ppermute(seg_loc, "tp", SWAP)])
        x_other = []
        for c in range(X_CHUNKS):
            x_other.append(lax.ppermute(x_loc[c * half:(c + 1) * half], "tp", SWAP))

        def project(x_rows, w):
            out = jnp.einsum("sd,dhe->she", x_rows, w, preferred_element_type=jnp.float32).astype(jnp.bfloat16)
            return out.transpose(1, 0, 2)

        def slices(val):
            return [lax.dynamic_slice_in_dim(val, (cp_rank ^ s) * n_grp, n_grp, axis=0) for s in range(N_CP)]

        def exchange(parts):
            out = [parts[0]] + [None] * (N_CP - 1)
            for s in (2, 3, 1):
                out[s] = lax.ppermute(parts[s], "cp", cp_perm(s))
            return out

        jobs = [(x_loc, w_k, False), (x_loc, w_v, False)]
        for c in range(X_CHUNKS):
            jobs += [(x_other[c], w, w is w_k) for w in (w_k, w_v, w_q)]
        spread = []
        held = x_c = None
        for i, (x_new, w, fresh) in enumerate(jobs):
            x_c = x_new if i == 0 or fresh else x_c
            if held is not None:
                x_c, held = lax.optimization_barrier((x_c, held))
                spread.append(exchange(held))
            val = project(x_c, w)
            held = slices(val)
        spread.append(exchange(held))
        ks = [spread[0]] + spread[2::3]
        vs = [spread[1]] + spread[3::3]
        qs = spread[4::3]

        seg_all = jnp.stack([seg_pair] + [lax.ppermute(seg_pair, "cp", cp_perm(s)) for s in range(1, N_CP)])
        starts = jnp.sum((seg_all.reshape(1, -1) < seg_all.reshape(-1, 1)).astype(jnp.int32), axis=1).reshape(N_CP, 2, rows)
        ranks = jnp.array([cp_rank ^ s for s in range(N_CP)])
        own_piece = jnp.where(tp_rank == 0, ranks, 2 * N_CP - 1 - ranks)
        other_piece = 2 * N_CP - 1 - own_piece

        def meta_of(kind, q_piece):
            first, last = starts[:, kind, 0], starts[:, kind, -1]
            k_full = jnp.minimum((last + PIECE - 1) // PIECE, q_piece)
            return jnp.concatenate([own_piece, other_piece, q_piece, first // PIECE, k_full]).astype(jnp.int32)

        k_chunks = [(0, 0, rows)] + [(1, c * half, half) for c in range(X_CHUNKS)]
        k_parts = [k[s] for s in range(N_CP) for k in ks]
        v_parts = [v[s] for s in range(N_CP) for v in vs]
        n_half = n_grp // HALVES
        meta_other = meta_of(1, other_piece)
        starts_other = starts[:, 1][:, None]
        q_parts = [q[s] for s in range(N_CP) for q in qs]
        back_other = [None] * (N_CP * HALVES)
        for hf in range(HALVES):
            o_half = attention(meta_other, starts_other, k_parts, v_parts, q_parts, k_chunks,
                               [(c * half, half) for c in range(X_CHUNKS)], coef, hf * n_half, n_half)
            o_slots = [o_half[s] for s in range(N_CP)]
            if hf + 1 < HALVES:
                meta_other, o_slots = lax.optimization_barrier((meta_other, o_slots))
            back_other[hf::HALVES] = exchange(o_slots)

        w_out = w_o.reshape(n_loc * head_dim, -1)
        groups = jnp.stack([ranks * HALVES + hf for hf in range(HALVES)], axis=1).reshape(-1).astype(jnp.int32)
        recvs = []
        part = None
        col0 = 0
        for n_cols in Y_SPLITS:
            if part is not None:
                groups, part = lax.optimization_barrier((groups, part))
                recvs.append(lax.ppermute(part, "tp", SWAP))
            part = out_proj(groups, back_other, w_out, col0, n_cols)
            col0 += n_cols
        x_own, part = lax.optimization_barrier((x_loc, part))
        recvs.append(lax.ppermute(part, "tp", SWAP))
        q_own = project(x_own, w_q)
        qs_own = exchange(slices(q_own))
        o_own = attention(meta_of(0, own_piece), starts[:, 0][:, None], k_parts, v_parts,
                          qs_own, k_chunks, [(0, rows)], coef, 0, n_grp)
        back_own = exchange([o_own[s] for s in range(N_CP)])
        own_groups = ranks.astype(jnp.int32)
        y = None
        col0 = 0
        for n_cols, recv in zip(Y_SPLITS, recvs):
            y = out_proj(own_groups, back_own, w_out, col0, n_cols, recv, y)
            col0 += n_cols
        return y

    return jax.shard_map(
        per_device,
        mesh=mesh,
        in_specs=(P(("dp", "cp", "tp"), None), P(("dp", "cp", "tp")), P(None, "tp", None), P(None, "tp", None), P(None, "tp", None), P("tp", None, None)),
        out_specs=P(("dp", "cp", "tp"), None),
        check_vma=False,
    )
```

time: 1300 us -> 1140 us (0.88)
  Pallas kernels: 395 us -> 311 us
  blocking collectives: 56 us -> 0 us
  starting transfers between devices: 158 us -> 112 us
  waiting for transfers between devices: 327 us -> 341 us
    pallas_call x20 -> x21, Pallas kernels: 395 us -> 311 us  [the longest x3 163 us: attention(): pl.pallas_call(functools.partial(attn_kernel, head0=head0, n_steps=n_step...]
    ppermute x9, waiting for transfers between devices: 218 us -> 135 us  [per_device(): recvs.append(lax.ppermute(part, 'tp', SWAP))]
    all_gather x1 -> x0, blocking collectives: 56 us -> none  [per_device(): lax.all_gather(seg_loc, ('cp', 'tp'), axis=0, tiled=True)]
    ppermute x33 -> x40, waiting for transfers between devices: 109 us -> 161 us  [the longest x36 161 us: exchange(): out[s] = lax.ppermute(parts[s], 'cp', cp_perm(s))]
    ppermute x9, starting transfers between devices: 128 us -> 80.1 us  [per_device(): recvs.append(lax.ppermute(part, 'tp', SWAP))]
    ppermute x2, waiting for transfers between devices: 0.01 us -> 44.1 us  [per_device(): x_other.append(lax.ppermute(x_loc[c * half:(c + 1) * half], 'tp', SWAP))]
    ppermute x33 -> x40, starting transfers between devices: 26.4 us -> 31 us  [the longest x36 25.5 us: exchange(): out[s] = lax.ppermute(parts[s], 'cp', cp_perm(s))]
  transfers between devices with their start and end apart: 44 -> 51, of which waited for: 16 -> 16; matrix products, arithmetic and copies ran while one was open for 23% -> 27% of each run, Pallas kernels for 17% -> 11%
where the time goes in v2:
time: 1140 us; the launch traced here: 1130 us
  waiting for transfers between devices  341 us (30%)
  Pallas kernels  311 us (27%)
  matrix products  300 us (26%)
  starting transfers between devices  112 us (10%)
  local copies, waits for them, and re-layouts  55.5 us (5%)
  other arithmetic  11.4 us (1%)
    dot_general x9, matrix products, project(): jnp.einsum('sd,dhe->she', x_rows, w, preferred_element_type=jnp.float32)  300 us
    pallas_call x3, Pallas kernels, attention(): pl.pallas_call(functools.partial(attn_kernel, head0=head0, n_steps=n_step...  163 us
    ppermute x36, waiting for transfers between devices, exchange(): out[s] = lax.ppermute(parts[s], 'cp', cp_perm(s))  161 us
    pallas_call x18, Pallas kernels, out_proj(): pl.pallas_call(functools.partial(out_kernel, n_parts=n_parts, has_recv=re...  148 us
    ppermute x9, waiting for transfers between devices, per_device(): recvs.append(lax.ppermute(part, 'tp', SWAP))  135 us
    ppermute x9, starting transfers between devices, per_device(): recvs.append(lax.ppermute(part, 'tp', SWAP))  80.1 us
    ppermute x2, waiting for transfers between devices, per_device(): x_other.append(lax.ppermute(x_loc[c * half:(c + 1) * half], 'tp', SWAP))  44.1 us
    ppermute x36, starting transfers between devices, exchange(): out[s] = lax.ppermute(parts[s], 'cp', cp_perm(s))  25.5 us
  transfers between devices with their start and end apart: 51, of which 16 were waited for; matrix products, arithmetic and copies ran while one was open for 27% of the time, Pallas kernels for 11%

profile of v2, /device:TPU:0, one launch (start us, length us, event | category | flops | bytes accessed | tf_op | source)
XLA Modules:
  0.0 1131.3 jit_solution(3910345110968095577)
XLA Ops:
  3.3 51.2 %fusion.27 = bf16[512,32,128]{2,0,1:T(8,128)(2,1)S(1)} fusion(bf16[8192,32,128]{2,1,0:T(8,128)(2,1)} %param.9, bf16[512,8192]{1,0:T(8,128)(2,1)} %param.6), kind=kOutput, calls=%fused_computation.28 | convolution fusion | flops 34361835520 | bytes 79691776 | tf_op jit(solution)/shard_map/sd,dhe->she/dot_general | solution.py:200
  65.5 40.6 %fusion.32 = bf16[512,32,128]{2,0,1:T(8,128)(2,1)S(1)} fusion(bf16[8192,32,128]{2,1,0:T(8,128)(2,1)} %param.10, bf16[512,8192]{1,0:T(8,128)(2,1)S(1)} %bitcast.161), kind=kOutput, calls=%fused_computation.29 | convolution fusion | flops 34361835520 | bytes 79691776 | tf_op jit(solution)/shard_map/sd,dhe->she/dot_general | solution.py:200
  113.7 44.1 %collective-permute-done.4 = bf16[256,8192]{1,0:T(8,128)(2,1)} collective-permute-done((bf16[256,8192]{1,0:T(8,128)(2,1)}, bf16[256,8192]{1,0:T(8,128)(2,1)}, u32[]{:S(2)}, u32[]{:S(2)}) %collective-permute-start.4) | collective-permute-done | bytes 4194336 | tf_op jit(solution)/shard_map/ppermute | solution.py:197
  157.8 27.0 %fusion.42 = bf16[256,32,128]{2,0,1:T(8,128)(2,1)S(1)} fusion(bf16[8192,32,128]{2,1,0:T(8,128)(2,1)} %param.9, bf16[256,8192]{1,0:T(8,128)(2,1)} %collective-permute-done.4), kind=kOutput, calls=%fused_computation.31 | convolution fusion | flops 17180917760 | bytes 73400320 | tf_op jit(solution)/shard_map/sd,dhe->she/dot_general | solution.py:200
  186.0 28.2 %fusion.52 = bf16[256,32,128]{2,0,1:T(8,128)(2,1)} fusion(bf16[8192,32,128]{2,1,0:T(8,128)(2,1)} %param.10, bf16[256,8192]{1,0:T(8,128)(2,1)} %collective-permute-done.4), kind=kOutput, calls=%fused_computation.33 | convolution fusion | flops 17180917760 | bytes 73400320 | tf_op jit(solution)/shard_map/sd,dhe->she/dot_general | solution.py:200
  217.0 28.2 %fusion.62 = bf16[256,32,128]{2,0,1:T(8,128)(2,1)} fusion(bf16[8192,32,128]{2,1,0:T(8,128)(2,1)} %param.8, bf16[256,8192]{1,0:T(8,128)(2,1)} %collective-permute-done.4), kind=kOutput, calls=%fused_computation.35 | convolution fusion | flops 17180917760 | bytes 73400320 | tf_op jit(solution)/shard_map/sd,dhe->she/dot_general | solution.py:200
  250.3 28.0 %fusion.47 = bf16[256,32,128]{2,0,1:T(8,128)(2,1)} fusion(bf16[8192,32,128]{2,1,0:T(8,128)(2,1)} %param.9, bf16[256,8192]{1,0:T(8,128)(2,1)} %collective-permute-done.5), kind=kOutput, calls=%fused_computation.32 | convolution fusion | flops 17180917760 | bytes 73400320 | tf_op jit(solution)/shard_map/sd,dhe->she/dot_general | solution.py:200
  285.5 28.5 %fusion.57 = bf16[256,32,128]{2,0,1:T(8,128)(2,1)} fusion(bf16[8192,32,128]{2,1,0:T(8,128)(2,1)} %param.10, bf16[256,8192]{1,0:T(8,128)(2,1)} %collective-permute-done.5), kind=kOutput, calls=%fused_computation.34 | convolution fusion | flops 17180917760 | bytes 73400320 | tf_op jit(solution)/shard_map/sd,dhe->she/dot_general | solution.py:200
  329.5 28.0 %fusion.67 = bf16[256,32,128]{2,0,1:T(8,128)(2,1)} fusion(bf16[8192,32,128]{2,1,0:T(8,128)(2,1)} %param.8, bf16[256,8192]{1,0:T(8,128)(2,1)} %collective-permute-done.5), kind=kOutput, calls=%fused_computation.36 | convolution fusion | flops 17180917760 | bytes 73400320 | tf_op jit(solution)/shard_map/sd,dhe->she/dot_general | solution.py:200
  375.9 44.9 %collective-permute-done.23.refs_23_ = bf16[8,256,128]{2,1,0:T(8,128)(2,1)S(1)} collective-permute-done((bf16[8,256,128]{2,1,0:T(8,128)(2,1)}, bf16[8,256,128]{2,1,0:T(8,128)(2,1)S(1)}, u32[]{:S(2)}, u32[]{:S(2)}) %collective-permute-start.23) | collective-permute-done | bytes 524320 | tf_op jit(solution)/shard_map/ppermute | solution.py:209
  447.4 54.2 %attention.3 = bf16[4,512,512]{2,1,0:T(8,128)(2,1)} custom-call(s32[20]{0:T(128)S(1)} %concatenate.37.meta_ref, s32[4,1,512]{2,1,0:T(1,128)S(1)} %get-tuple-element.180.start_ref, bf16[8,512,128]{2,1,0:T(8,128)(2,1)} %get-tuple-element.63.refs_0_, bf16[8,256,128]{2,1,0:T(8,128)(2,1)S(1)} %get-tuple-element.66.refs_1_, ...), custom_call_target="tpu_custom_call" | custom-call | flops 15000000512 | bytes 15728640 | tf_op jit(solution)/shard_map/attention/pallas_call | solution.py:114
  504.4 54.6 %attention.4 = bf16[4,512,512]{2,1,0:T(8,128)(2,1)} custom-call(s32[20]{0:T(128)S(1)} %concatenate.37.meta_ref, s32[4,1,512]{2,1,0:T(1,128)S(1)} %get-tuple-element.180.start_ref, bf16[8,512,128]{2,1,0:T(8,128)(2,1)} %get-tuple-element.63.refs_0_, bf16[8,256,128]{2,1,0:T(8,128)(2,1)S(1)} %get-tuple-element.66.refs_1_, ...), custom_call_target="tpu_custom_call" | custom-call | flops 15000000512 | bytes 15728640 | tf_op jit(solution)/shard_map/attention/pallas_call | solution.py:114
  687.6 40.6 %fusion.37 = bf16[512,32,128]{2,0,1:T(8,128)(2,1)S(1)} fusion(bf16[8192,32,128]{2,1,0:T(8,128)(2,1)} %param.8, bf16[512,8192]{1,0:T(8,128)(2,1)S(1)} %copy-done.26), kind=kOutput, calls=%fused_computation.30 | convolution fusion | flops 34361835520 | bytes 79691776 | tf_op jit(solution)/shard_map/sd,dhe->she/dot_general | solution.py:200
  734.5 21.8 %collective-permute-done.38.refs_27_ = bf16[8,512,128]{2,1,0:T(8,128)(2,1)} collective-permute-done((bf16[8,512,128]{2,1,0:T(8,128)(2,1)}, bf16[8,512,128]{2,1,0:T(8,128)(2,1)}, u32[]{:S(2)}, u32[]{:S(2)}) %collective-permute-start.38) | collective-permute-done | bytes 1048608 | tf_op jit(solution)/shard_map/ppermute | solution.py:209
  756.2 21.8 %collective-permute-done.37.refs_26_ = bf16[8,512,128]{2,1,0:T(8,128)(2,1)} collective-permute-done((bf16[8,512,128]{2,1,0:T(8,128)(2,1)}, bf16[8,512,128]{2,1,0:T(8,128)(2,1)}, u32[]{:S(2)}, u32[]{:S(2)}) %collective-permute-start.37) | collective-permute-done | bytes 1048608 | tf_op jit(solution)/shard_map/ppermute | solution.py:209
  786.4 54.4 %attention.5 = bf16[4,512,1024]{2,1,0:T(8,128)(2,1)} custom-call(s32[20]{0:T(128)S(1)} %concatenate.31.meta_ref, s32[4,1,512]{2,1,0:T(1,128)S(1)} %get-tuple-element.181.start_ref, bf16[8,512,128]{2,1,0:T(8,128)(2,1)} %get-tuple-element.63.refs_0_, bf16[8,256,128]{2,1,0:T(8,128)(2,1)S(1)} %copy-done.6, bf16[8,256,128]{2,1,0:T(8,128)(2,1)S(1)} %copy-done.10, ...), custom_call_target="tpu_custom_call" | custom-call | flops 15000000512 | bytes 15728640 | tf_op jit(solution)/shard_map/attention/pallas_call | solution.py:114
  845.4 30.8 %collective-permute-start.47 = (f32[512,1024]{1,0:T(8,128)}, f32[512,1024]{1,0:T(8,128)}, u32[]{:S(2)}, u32[]{:S(2)}) collective-permute-start(f32[512,1024]{1,0:T(8,128)} %out_proj.21), channel_id=1, source_target_pairs={{0,4},{4,0},{1,5},{5,1},{2,6},{6,2},{3,7},{7,3}} | collective-permute-start | bytes 6291464 | tf_op jit(solution)/shard_map/ppermute | solution.py:264
  876.9 23.9 %collective-permute-start.46 = (f32[512,1024]{1,0:T(8,128)}, f32[512,1024]{1,0:T(8,128)}, u32[]{:S(2)}, u32[]{:S(2)}) collective-permute-start(f32[512,1024]{1,0:T(8,128)} %out_proj.22), channel_id=1, source_target_pairs={{0,4},{4,0},{1,5},{5,1},{2,6},{6,2},{3,7},{7,3}} | collective-permute-start | bytes 6291464 | tf_op jit(solution)/shard_map/ppermute | solution.py:264
  900.8 21.4 %collective-permute-start.45 = (f32[512,1024]{1,0:T(8,128)}, f32[512,1024]{1,0:T(8,128)}, u32[]{:S(2)}, u32[]{:S(2)}) collective-permute-start(f32[512,1024]{1,0:T(8,128)} %out_proj.23), channel_id=1, source_target_pairs={{0,4},{4,0},{1,5},{5,1},{2,6},{6,2},{3,7},{7,3}} | collective-permute-start | bytes 6291464 | tf_op jit(solution)/shard_map/ppermute | solution.py:264
  955.2 12.4 %collective-permute-done.46.refs_8_ = f32[512,1024]{1,0:T(8,128)} collective-permute-done((f32[512,1024]{1,0:T(8,128)}, f32[512,1024]{1,0:T(8,128)}, u32[]{:S(2)}, u32[]{:S(2)}) %collective-permute-start.46) | collective-permute-done | bytes 2097184 | tf_op jit(solution)/shard_map/ppermute | solution.py:264
  976.3 36.3 %collective-permute-done.45.refs_8_ = f32[512,1024]{1,0:T(8,128)} collective-permute-done((f32[512,1024]{1,0:T(8,128)}, f32[512,1024]{1,0:T(8,128)}, u32[]{:S(2)}, u32[]{:S(2)}) %collective-permute-start.45) | collective-permute-done | bytes 2097184 | tf_op jit(solution)/shard_map/ppermute | solution.py:264
  1021.2 36.3 %collective-permute-done.44.refs_8_ = f32[512,1024]{1,0:T(8,128)} collective-permute-done((f32[512,1024]{1,0:T(8,128)}, f32[512,1024]{1,0:T(8,128)}, u32[]{:S(2)}, u32[]{:S(2)}) %collective-permute-start.44) | collective-permute-done | bytes 2097184 | tf_op jit(solution)/shard_map/ppermute | solution.py:264
  1066.2 36.3 %collective-permute-done.43.refs_8_ = f32[512,1024]{1,0:T(8,128)} collective-permute-done((f32[512,1024]{1,0:T(8,128)}, f32[512,1024]{1,0:T(8,128)}, u32[]{:S(2)}, u32[]{:S(2)}) %collective-permute-start.43) | collective-permute-done | bytes 2097184 | tf_op jit(solution)/shard_map/ppermute | solution.py:264
  1111.1 13.9 %collective-permute-done.42.refs_8_ = f32[512,512]{1,0:T(8,128)} collective-permute-done((f32[512,512]{1,0:T(8,128)}, f32[512,512]{1,0:T(8,128)}, u32[]{:S(2)}, u32[]{:S(2)}) %collective-permute-start.42) | collective-permute-done | bytes 1048608 | tf_op jit(solution)/shard_map/ppermute | solution.py:268
  (215 shorter events, 323.3 us)
Async XLA Ops:
  0.0 106.1 %collective-permute-start = (s32[512]{0:T(512)}, s32[512]{0:T(512)}, u32[]{:S(2)}, u32[]{:S(2)}) collective-permute-start(s32[512]{0:T(512)} %param.7), channel_id=1, source_target_pairs={{0,4},{4,0},{1,5},{5,1},{2,6},{6,2},{3,7},{7,3}} | collective-permute-start | bytes 6152 | tf_op jit(solution)/shard_map/ppermute | solution.py:194
  56.6 193.0 %collective-permute-start.6 = (bf16[8,512,128]{2,1,0:T(8,128)(2,1)}, bf16[8,512,128]{2,1,0:T(8,128)(2,1)}, u32[]{:S(2)}, u32[]{:S(2)}) collective-permute-start(bf16[8,512,128]{2,1,0:T(8,128)(2,1)} %get-tuple-element.71), channel_id=1, source_target_pairs={{0,1},{1,0},{2,3},{3,2},{4,5},{5,4},{6,7},{7,6}} | collective-permute-start | bytes 3145736 | tf_op jit(solution)/shard_map/ppermute | solution.py:209
  64.0 93.8 %collective-permute-start.4 = (bf16[256,8192]{1,0:T(8,128)(2,1)}, bf16[256,8192]{1,0:T(8,128)(2,1)}, u32[]{:S(2)}, u32[]{:S(2)}) collective-permute-start(bf16[256,8192]{1,0:T(8,128)(2,1)} %get-tuple-element.131), channel_id=1, source_target_pairs={{0,4},{4,0},{1,5},{5,1},{2,6},{6,2},{3,7},{7,3}} | collective-permute-start | bytes 12582920 | tf_op jit(solution)/shard_map/ppermute | solution.py:197
  111.0 138.8 %collective-permute-start.9 = (bf16[8,512,128]{2,1,0:T(8,128)(2,1)}, bf16[8,512,128]{2,1,0:T(8,128)(2,1)}, u32[]{:S(2)}, u32[]{:S(2)}) collective-permute-start(bf16[8,512,128]{2,1,0:T(8,128)(2,1)} %get-tuple-element.74), channel_id=1, source_target_pairs={{0,2},{1,3},{2,0},{3,1},{4,6},{5,7},{6,4},{7,5}} | collective-permute-start | bytes 3145736 | tf_op jit(solution)/shard_map/ppermute | solution.py:209
  112.5 168.5 %collective-permute-start.12 = (bf16[8,512,128]{2,1,0:T(8,128)(2,1)}, bf16[8,512,128]{2,1,0:T(8,128)(2,1)}, u32[]{:S(2)}, u32[]{:S(2)}) collective-permute-start(bf16[8,512,128]{2,1,0:T(8,128)(2,1)} %get-tuple-element.77), channel_id=1, source_target_pairs={{0,3},{1,2},{2,1},{3,0},{4,7},{5,6},{6,5},{7,4}} | collective-permute-start | bytes 3145736 | tf_op jit(solution)/shard_map/ppermute | solution.py:209
  112.5 135.6 %collective-permute-start.5 = (bf16[256,8192]{1,0:T(8,128)(2,1)}, bf16[256,8192]{1,0:T(8,128)(2,1)}, u32[]{:S(2)}, u32[]{:S(2)}) collective-permute-start(bf16[256,8192]{1,0:T(8,128)(2,1)} %get-tuple-element.130), channel_id=1, source_target_pairs={{0,4},{4,0},{1,5},{5,1},{2,6},{6,2},{3,7},{7,3}} | collective-permute-start | bytes 12582920 | tf_op jit(solution)/shard_map/ppermute | solution.py:197
  186.0 96.5 %collective-permute-start.7 = (bf16[8,256,128]{2,1,0:T(8,128)(2,1)}, bf16[8,256,128]{2,1,0:T(8,128)(2,1)S(1)}, u32[]{:S(2)}, u32[]{:S(2)}) collective-permute-start(bf16[8,256,128]{2,1,0:T(8,128)(2,1)} %get-tuple-element.72), channel_id=1, source_target_pairs={{0,1},{1,0},{2,3},{3,2},{4,5},{5,4},{6,7},{7,6}} | collective-permute-start | bytes 1572872 | tf_op jit(solution)/shard_map/ppermute | solution.py:209
  361.2 83.0 %collective-permute-start.15 = (bf16[8,512,128]{2,1,0:T(8,128)(2,1)}, bf16[8,512,128]{2,1,0:T(8,128)(2,1)}, u32[]{:S(2)}, u32[]{:S(2)}) collective-permute-start(bf16[8,512,128]{2,1,0:T(8,128)(2,1)} %get-tuple-element.84), channel_id=1, source_target_pairs={{0,1},{1,0},{2,3},{3,2},{4,5},{5,4},{6,7},{7,6}} | collective-permute-start | bytes 3145736 | tf_op jit(solution)/shard_map/ppermute | solution.py:209
  362.6 81.6 %collective-permute-start.18 = (bf16[8,512,128]{2,1,0:T(8,128)(2,1)}, bf16[8,512,128]{2,1,0:T(8,128)(2,1)}, u32[]{:S(2)}, u32[]{:S(2)}) collective-permute-start(bf16[8,512,128]{2,1,0:T(8,128)(2,1)} %get-tuple-element.87), channel_id=1, source_target_pairs={{0,2},{1,3},{2,0},{3,1},{4,6},{5,7},{6,4},{7,5}} | collective-permute-start | bytes 3145736 | tf_op jit(solution)/shard_map/ppermute | solution.py:209
  363.2 81.1 %collective-permute-start.21 = (bf16[8,512,128]{2,1,0:T(8,128)(2,1)}, bf16[8,512,128]{2,1,0:T(8,128)(2,1)}, u32[]{:S(2)}, u32[]{:S(2)}) collective-permute-start(bf16[8,512,128]{2,1,0:T(8,128)(2,1)} %get-tuple-element.90), channel_id=1, source_target_pairs={{0,3},{1,2},{2,1},{3,0},{4,7},{5,6},{6,5},{7,4}} | collective-permute-start | bytes 3145736 | tf_op jit(solution)/shard_map/ppermute | solution.py:209
  364.0 56.7 %collective-permute-start.23 = (bf16[8,256,128]{2,1,0:T(8,128)(2,1)}, bf16[8,256,128]{2,1,0:T(8,128)(2,1)S(1)}, u32[]{:S(2)}, u32[]{:S(2)}) collective-permute-start(bf16[8,256,128]{2,1,0:T(8,128)(2,1)} %get-tuple-element.92), channel_id=1, source_target_pairs={{0,3},{1,2},{2,1},{3,0},{4,7},{5,6},{6,5},{7,4}} | collective-permute-start | bytes 1572872 | tf_op jit(solution)/shard_map/ppermute | solution.py:209
  364.9 67.1 %collective-permute-start.29 = (bf16[8,256,128]{2,1,0:T(8,128)(2,1)}, bf16[8,256,128]{2,1,0:T(8,128)(2,1)}, u32[]{:S(2)}, u32[]{:S(2)}) collective-permute-start(bf16[8,256,128]{2,1,0:T(8,128)(2,1)} %get-tuple-element.156), channel_id=1, source_target_pairs={{0,3},{1,2},{2,1},{3,0},{4,7},{5,6},{6,5},{7,4}} | collective-permute-start | bytes 1572872 | tf_op jit(solution)/shard_map/ppermute | solution.py:209
  731.1 46.9 %collective-permute-start.37 = (bf16[8,512,128]{2,1,0:T(8,128)(2,1)}, bf16[8,512,128]{2,1,0:T(8,128)(2,1)}, u32[]{:S(2)}, u32[]{:S(2)}) collective-permute-start(bf16[8,512,128]{2,1,0:T(8,128)(2,1)} %get-tuple-element.137), channel_id=1, source_target_pairs={{0,2},{1,3},{2,0},{3,1},{4,6},{5,7},{6,4},{7,5}} | collective-permute-start | bytes 3145736 | tf_op jit(solution)/shard_map/ppermute | solution.py:209
  731.6 46.5 %collective-permute-start.36 = (bf16[8,512,128]{2,1,0:T(8,128)(2,1)}, bf16[8,512,128]{2,1,0:T(8,128)(2,1)}, u32[]{:S(2)}, u32[]{:S(2)}) collective-permute-start(bf16[8,512,128]{2,1,0:T(8,128)(2,1)} %get-tuple-element.138), channel_id=1, source_target_pairs={{0,1},{1,0},{2,3},{3,2},{4,5},{5,4},{6,7},{7,6}} | collective-permute-start | bytes 3145736 | tf_op jit(solution)/shard_map/ppermute | solution.py:209
  732.4 112.9 %collective-permute-start.50 = (f32[512,512]{1,0:T(8,128)S(1)}, f32[512,512]{1,0:T(8,128)S(1)}, u32[]{:S(2)}, u32[]{:S(2)}) collective-permute-start(f32[512,512]{1,0:T(8,128)S(1)} %copy-done.4), channel_id=1, source_target_pairs={{0,4},{4,0},{1,5},{5,1},{2,6},{6,2},{3,7},{7,3}} | collective-permute-start | bytes 3145736 | tf_op jit(solution)/shard_map/ppermute | solution.py:264
  732.4 143.8 %collective-permute-start.48 = (f32[512,1024]{1,0:T(8,128)}, f32[512,1024]{1,0:T(8,128)S(1)}, u32[]{:S(2)}, u32[]{:S(2)}) collective-permute-start(f32[512,1024]{1,0:T(8,128)} %copy-done.2), channel_id=1, source_target_pairs={{0,4},{4,0},{1,5},{5,1},{2,6},{6,2},{3,7},{7,3}} | collective-permute-start | bytes 6291464 | tf_op jit(solution)/shard_map/ppermute | solution.py:264
  756.2 171.8 %collective-permute-start.49 = (f32[512,1024]{1,0:T(8,128)S(1)}, f32[512,1024]{1,0:T(8,128)S(1)}, u32[]{:S(2)}, u32[]{:S(2)}) collective-permute-start(f32[512,1024]{1,0:T(8,128)S(1)} %copy-done.1), channel_id=1, source_target_pairs={{0,4},{4,0},{1,5},{5,1},{2,6},{6,2},{3,7},{7,3}} | collective-permute-start | bytes 6291464 | tf_op jit(solution)/shard_map/ppermute | solution.py:264
  844.5 56.3 %collective-permute-start.40 = (bf16[512,1024]{1,0:T(8,128)(2,1)S(1)}, bf16[512,1024]{1,0:T(8,128)(2,1)S(1)}, u32[]{:S(2)}, u32[]{:S(2)}) collective-permute-start(bf16[512,1024]{1,0:T(8,128)(2,1)S(1)} %get-tuple-element.133), channel_id=1, source_target_pairs={{0,2},{1,3},{2,0},{3,1},{4,6},{5,7},{6,4},{7,5}} | collective-permute-start | bytes 3145736 | tf_op jit(solution)/shard_map/ppermute | solution.py:209
  845.4 101.2 %collective-permute-start.47 = (f32[512,1024]{1,0:T(8,128)}, f32[512,1024]{1,0:T(8,128)}, u32[]{:S(2)}, u32[]{:S(2)}) collective-permute-start(f32[512,1024]{1,0:T(8,128)} %out_proj.21), channel_id=1, source_target_pairs={{0,4},{4,0},{1,5},{5,1},{2,6},{6,2},{3,7},{7,3}} | collective-permute-start | bytes 6291464 | tf_op jit(solution)/shard_map/ppermute | solution.py:264
  876.9 90.8 %collective-permute-start.46 = (f32[512,1024]{1,0:T(8,128)}, f32[512,1024]{1,0:T(8,128)}, u32[]{:S(2)}, u32[]{:S(2)}) collective-permute-start(f32[512,1024]{1,0:T(8,128)} %out_proj.22), channel_id=1, source_target_pairs={{0,4},{4,0},{1,5},{5,1},{2,6},{6,2},{3,7},{7,3}} | collective-permute-start | bytes 6291464 | tf_op jit(solution)/shard_map/ppermute | solution.py:264
  900.8 111.8 %collective-permute-start.45 = (f32[512,1024]{1,0:T(8,128)}, f32[512,1024]{1,0:T(8,128)}, u32[]{:S(2)}, u32[]{:S(2)}) collective-permute-start(f32[512,1024]{1,0:T(8,128)} %out_proj.23), channel_id=1, source_target_pairs={{0,4},{4,0},{1,5},{5,1},{2,6},{6,2},{3,7},{7,3}} | collective-permute-start | bytes 6291464 | tf_op jit(solution)/shard_map/ppermute | solution.py:264
  922.1 135.4 %collective-permute-start.44 = (f32[512,1024]{1,0:T(8,128)}, f32[512,1024]{1,0:T(8,128)}, u32[]{:S(2)}, u32[]{:S(2)}) collective-permute-start(f32[512,1024]{1,0:T(8,128)} %out_proj.24), channel_id=1, source_target_pairs={{0,4},{4,0},{1,5},{5,1},{2,6},{6,2},{3,7},{7,3}} | collective-permute-start | bytes 6291464 | tf_op jit(solution)/shard_map/ppermute | solution.py:264
  928.0 174.5 %collective-permute-start.43 = (f32[512,1024]{1,0:T(8,128)}, f32[512,1024]{1,0:T(8,128)}, u32[]{:S(2)}, u32[]{:S(2)}) collective-permute-start(f32[512,1024]{1,0:T(8,128)} %out_proj.25), channel_id=1, source_target_pairs={{0,4},{4,0},{1,5},{5,1},{2,6},{6,2},{3,7},{7,3}} | collective-permute-start | bytes 6291464 | tf_op jit(solution)/shard_map/ppermute | solution.py:264
  946.6 178.4 %collective-permute-start.42 = (f32[512,512]{1,0:T(8,128)}, f32[512,512]{1,0:T(8,128)}, u32[]{:S(2)}, u32[]{:S(2)}) collective-permute-start(f32[512,512]{1,0:T(8,128)} %out_proj.26), channel_id=1, source_target_pairs={{0,4},{4,0},{1,5},{5,1},{2,6},{6,2},{3,7},{7,3}} | collective-permute-start | bytes 3145736 | tf_op jit(solution)/shard_map/ppermute | solution.py:268
  (65 other events, 2250.9 us)
